TPU v7x, 32 devices: a whole 2x2x4 slice. The times are simulated.
32 devices in a mesh: frag: 2 (over x), occ: 2 (over core), vir: 8 (over z, y).
Axes of the slice: x: 2, y: 2, z: 4, core: 2. Of those that a mesh axis runs over, the one named last changes fastest.
Arguments:
- factors: bfloat16 [8, 1024, 3072], P(('frag', 'occ'), 'vir'), parts along dimension 0, may hold values from -2 to 2
- occ_energy: int32 [8], P('frag'), parts along dimension 0, may hold values from -1536 to -512
- vir_energy: int32 [2048], P('frag'), parts along dimension 0, may hold values from 512 to 4096
Outputs:
- density: float32 [8, 1024, 3072], P(('frag', 'occ'), 'vir'), parts along dimension 0
There are 2 independent parts, one for each index of `frag`. A program takes and returns all parts, laid end to end along the dimension named above; each array names one. Nothing has to cross between parts.
Inputs may be any that keep to these rules, and one draw needn't show every extreme that they name: `occ_energy`: occupied energies lie at or below the highest occupied level -512. `vir_energy`: virtual energies lie at or above the lowest virtual level 512.
All inputs are finite; a program needn't handle non-finite values.
Results may differ from a plain program's by a relative error of at most 0.0055.
Values may be sent and summed in bfloat16 or wider, within the bound.
No kernel may reach another device: no remote copies, remote signals or barrier semaphores. Data moves between devices by JAX's collectives and lax.ppermute only.
A program may use at most 128 MiB of HBM per device.

v0:
```python
import functools

import jax
import jax.numpy as jnp
import numpy as np
from jax import lax
from jax.experimental import pallas as pl
from jax.experimental.pallas import tpu as pltpu
from jax.sharding import PartitionSpec as P

energy_unit = 1.0 / 1024.0


last_cuts = 2
body_steps = 2
body_tiles = 3
last_tiles = 6

across = (((1,), (1,)), ((), ()))
along = (((1,), (0,)), ((), ()))


def ring_order(mesh, axis):
    devices = mesh.devices
    for name in reversed(mesh.axis_names):
        if name != axis:
            devices = devices[(slice(None),) * mesh.axis_names.index(name) + (0,)]
    count = len(devices)
    spots = [tuple(getattr(device, "coords", ())) for device in devices]
    widths = [len(set(values)) for values in zip(*spots)] if all(spots) else []
    if sorted(widths)[-2:-1] == [2] and sorted(widths)[-1] * 2 == count:
        long = max(range(len(widths)), key=lambda d: widths[d])
        short = [d for d in range(len(widths)) if widths[d] == 2 and d != long][0]
        low = min(spot[short] for spot in spots)
        there = sorted((k for k in range(count) if spots[k][short] == low), key=lambda k: spots[k][long])
        back = sorted((k for k in range(count) if spots[k][short] != low), key=lambda k: -spots[k][long])
        return there + back
    return list(range(count))


def cut_kernel(source, *refs):
    *pieces, sems = refs
    slabs, local, rows, slab = pieces[0].shape
    copies = []
    for k, piece in enumerate(pieces):
        for i in range(local):
            for q in range(slabs):
                place = source.at[i, pl.ds(k * rows, rows), pl.ds(q * slab, slab)]
                copies.append(pltpu.make_async_copy(place, piece.at[q, i], sems.at[len(copies)]))
    for copy in copies:
        copy.start()
    for copy in copies:
        copy.wait()


def cut(source, count):
    local, rows, aux = source.shape
    slab = 128 * max(k for k in range(1, 3) if aux % (128 * k) == 0)
    slabs = aux // slab
    vmem = pl.BlockSpec(memory_space=pltpu.VMEM)
    return pl.pallas_call(
        cut_kernel,
        out_shape=[jax.ShapeDtypeStruct((slabs, local, rows // count, slab), source.dtype)] * count,
        in_specs=[pl.BlockSpec(memory_space=pltpu.HBM)],
        out_specs=[vmem] * count,
        scratch_shapes=[pltpu.SemaphoreType.DMA((count * local * slabs,))],
        compiler_params=pltpu.CompilerParams(vmem_limit_bytes=8 * 1024 * 1024),
        name="cut",
    )(source)


def block_kernel(layout, occ_pairs, own_vir, vir_rows, *refs):
    number, parts, owned, count, steps, tiles, prior, stage = layout
    refs = list(refs)
    own = [[refs.pop(0) for _ in range(owned)] for _ in range(1 if stage == 2 else parts)]
    if number:
        groups = [[refs.pop(0) for _ in range(count)] for _ in range(1 if stage == 1 else parts)]
    else:
        groups = own
    near_amplitude, near_swapped, held = (refs.pop(0) for _ in range(3)) if stage == 2 else (None, None, None)
    density_in = refs.pop(0) if prior and stage != 2 else None
    if stage == 1:
        amplitude, swapped_out, density, direct, in_sem = refs
    else:
        density_out, direct, amplitude, density, out_sem, in_sem = refs
    slabs, local, _, slab = own[0][0].shape
    rows = sum(piece.shape[2] for piece in own[0])
    width = sum(piece.shape[2] for piece in groups[0])
    wide, span = local * rows, local * width
    total = parts * local
    step = slabs * slab // tiles
    fresh = [part for part in range(len(groups)) if part or stage != 2]
    starts = {part: (0 if part == 0 else ((parts if stage != 2 else 0) + part - 1) * wide) for part in fresh}

    def tile_copy(start, inward):
        columns = pl.ds(start * step, step)
        if inward:
            return pltpu.make_async_copy(density_in.at[:, :, columns], density.at[:, :, columns], in_sem.at[start])
        return pltpu.make_async_copy(density.at[:, :, columns], density_out.at[:, :, columns], out_sem.at[start])

    if density_in is not None:
        for start in range(tiles):
            tile_copy(start, True).start()

    def stack(arrays, axis=0):
        return jnp.concatenate(arrays, axis=axis) if len(arrays) > 1 else arrays[0]

    def lines(group, first, number_of):
        return [
            stack([piece[first + q, k] for q in range(number_of)], 1) for k in range(local) for piece in group
        ]

    def depth_step(k, carry):
        some = slabs // steps
        all_rows = stack([line for block in own for line in lines(block, k * some, some)])
        for part in fresh:
            left = all_rows if part == 0 else all_rows[:wide]
            right = stack(lines(groups[part], k * some, some))
            term = lax.dot_general(left, right, across, preferred_element_type=jnp.float32)
            at = pl.ds(starts[part], left.shape[0])
            direct[at, :] = direct[at, :] + term
        return carry

    direct[...] = jnp.zeros_like(direct)
    lax.fori_loop(0, steps, depth_step, 0)
    vir_pair = own_vir[...] + vir_rows[number][:, :width]

    def tile(row, column, array=direct):
        sums = array[row * rows : (row + 1) * rows, column * width : (column + 1) * width]
        return sums.astype(jnp.bfloat16).astype(jnp.float32)

    for i in range(local):
        for part in fresh:
            for k in range(local):
                j = part * local + k
                divisor = (occ_pairs[i * total + j][:, :width] - vir_pair).astype(jnp.float32) * energy_unit
                straight = tile(starts[part] // rows + i, k)
                crossed = tile(j - local, i, near_swapped) if stage == 2 else tile(j, i)
                here = slice(j * width, (j + 1) * width)
                top = 2.0 * straight - crossed
                amplitude[i * rows : (i + 1) * rows, here] = (top / divisor).astype(jnp.bfloat16)
    if density_in is not None:
        for start in range(tiles):
            tile_copy(start, True).wait()
    if stage == 1:
        swapped_out[...] = direct[wide:, :].astype(jnp.bfloat16)
        return
    if stage == 2:
        amplitude[:, :span] = near_amplitude[...]
    prior_ref = held if stage == 2 else density if density_in is not None else None
    for start in range(tiles):
        columns = slice(start * step, (start + 1) * step)
        some = slabs // tiles
        factor = stack([line for group in groups for line in lines(group, start * some, some)])
        term = lax.dot_general(amplitude[...], factor, along, preferred_element_type=jnp.float32)
        term = term.reshape(local, rows, step)
        density[:, :, columns] = term if prior_ref is None else prior_ref[:, :, columns] + term
        tile_copy(start, False).start()
    for start in range(tiles):
        tile_copy(start, False).wait()


def block_step(number, energies, own, pieces, density, stage=None, near=()):
    parts = len(own)
    slabs, local, _, slab = own[0][0].shape
    rows = sum(piece.shape[2] for piece in own[0])
    vmem = pl.BlockSpec(memory_space=pltpu.VMEM)
    hbm = pl.BlockSpec(memory_space=pltpu.HBM)
    groups = 1 if stage == 1 else parts
    own = own[:1] if stage == 2 else own
    operands = [*energies, *[piece for block in own for piece in block], *pieces, *near]
    specs = [vmem] * len(operands)
    wide, aux = local * rows, slabs * slab
    span = local * sum(piece.shape[2] for piece in pieces) // groups if pieces else wide
    tiles = max(k for k in range(1, (last_tiles if stage == 2 else body_tiles) + 1) if slabs % k == 0)
    steps = 1 if stage == 1 else max(k for k in range(1, body_steps + 1) if slabs % k == 0)
    lines = {None: 2 * parts - 1, 1: parts, 2: parts - 1}[stage]
    prior = density is not None
    layout = (number, parts, len(own[0]), len(pieces) // groups, steps, tiles, prior, stage)
    scratch = [pltpu.VMEM((lines * wide, span), jnp.float32)]
    out_shape = jax.ShapeDtypeStruct((local, rows, aux), jnp.float32)
    out_specs = hbm
    aliases = {}
    if prior:
        if stage is None:
            aliases = {len(operands): 0}
        operands.append(density)
        specs.append(hbm)
    if stage == 1:
        out_shape = [
            jax.ShapeDtypeStruct((wide, span), jnp.bfloat16),
            jax.ShapeDtypeStruct(((parts - 1) * wide, span), jnp.bfloat16),
            out_shape,
        ]
        out_specs = [vmem] * 3
    else:
        scratch += [
            pltpu.VMEM((wide, parts * span), jnp.bfloat16),
            pltpu.VMEM((local, rows, aux), jnp.float32),
            pltpu.SemaphoreType.DMA((tiles,)),
        ]
    scratch.append(pltpu.SemaphoreType.DMA((tiles,)))
    products = lines + (0 if stage == 1 else parts)
    return pl.pallas_call(
        functools.partial(block_kernel, layout),
        out_shape=out_shape,
        in_specs=specs,
        out_specs=out_specs,
        scratch_shapes=scratch,
        input_output_aliases=aliases,
        compiler_params=pltpu.CompilerParams(vmem_limit_bytes=24 * 1024 * 1024),
        cost_estimate=pl.CostEstimate(
            flops=2 * products * wide * span * aux,
            bytes_accessed=2 * (parts * (span + wide) + 4 * wide) * aux,
            transcendentals=0,
        ),
    )(*operands)


def on_device(order, parts, factors, occ_energy, vir_energy):
    local, rows, _ = factors.shape
    count = len(order)
    halves = 2
    core = lax.axis_index("occ")
    place = lax.axis_index("vir")
    onward = [(order[k], order[(k + 1) % count]) for k in range(count)]
    backward = [(target, source) for source, target in onward]
    links = (onward, backward)
    near_core = [[((k + shift) % parts, k) for k in range(parts)] for shift in range(1, parts)]

    first = cut(factors, halves)
    half = rows // halves
    held = [{}, {}]
    own = [first]
    own += [[lax.ppermute(piece, "occ", pairs) for piece in first] for pairs in near_core]
    blocks, shifts, ranges = [], [], []
    for step in range(1, count - 1 + last_cuts):
        at = min(step, count - 1)
        some = half // last_cuts if at == count - 1 else half
        distance = (at + 1) // 2
        begins = [half * ((at - 1 + way) % 2) + some * (step - at) for way in range(2)]
        shifts.append([-distance, distance])
        ranges.append([np.arange(begin, begin + some) for begin in begins])
        for way in range(2):
            source = held[way][at - 2] if at > 2 else first[(at - 1 + way) % 2]
            if some < half:
                source = lax.slice_in_dim(source, some * (step - at), some * (step - at + 1), axis=2)
            held[way][step] = lax.ppermute(source, "vir", links[way])
        arrived = [held[way][step] for way in range(2)]
        block = list(arrived)
        for pairs in near_core:
            for way in range(2):
                block.append(lax.ppermute(arrived[way], "occ", pairs))
        blocks.append(block)

    spots = jnp.asarray([order.index(k) for k in range(count)], jnp.int32)
    away = np.zeros((len(blocks) + 1, rows), np.int32)
    inner = np.tile(np.arange(rows, dtype=np.int32), (len(blocks) + 1, 1))
    for number, (pair, spans) in enumerate(zip(shifts, ranges), 1):
        line = np.concatenate([np.full(len(span), shift) for shift, span in zip(pair, spans)])
        away[number, : len(line)] = line
        inner[number, : len(line)] = np.concatenate(spans)
    sources = jnp.asarray(order, jnp.int32)[(spots[place] + jnp.arange(-count, count, dtype=jnp.int32)) % count]
    energy_table = vir_energy.reshape(count, rows)[sources]
    vir_rows = energy_table[away + count, inner][:, None, :]
    own_vir = lax.dynamic_slice_in_dim(vir_energy, place * rows, rows)[:, None]
    mine_first = jnp.roll(occ_energy, -core * local)
    occ_pairs = (mine_first[:local, None] + mine_first[None, :]).reshape(-1, 1, 1)
    energies = (jnp.broadcast_to(occ_pairs, occ_pairs.shape[:2] + (rows,)), own_vir, vir_rows)

    density = block_step(0, energies, own, [], None)
    for number, block in enumerate(blocks, 1):
        if number < len(blocks):
            density = block_step(number, energies, own, block, density)
        else:
            near = block_step(number, energies, own, block[: len(links)], density, 1)
            density = block_step(number, energies, own, block, None, 2, near)
    return density


def solution(mesh):
    order = ring_order(mesh, "vir")
    parts = mesh.shape["occ"]

    def whole_step(factors, occ_energy, vir_energy):
        return on_device(order, parts, factors, occ_energy, vir_energy)

    return jax.shard_map(
        whole_step,
        mesh=mesh,
        in_specs=(P(("frag", "occ"), "vir", None), P("frag"), P("frag")),
        out_specs=P(("frag", "occ"), "vir", None),
        check_vma=False,
    )
```

profile of v0, /device:TPU:0, one launch (start us, length us, event | category | flops | bytes accessed | tf_op | source)
XLA Modules:
  0.0 170.8 jit_solution(4162933986420689650)
XLA Ops:
  0.0 1.4 copy-done.1
  1.4 0.8 cut.1
  2.2 0.6 collective-permute-start.10
  2.8 2.6 %collective-permute-start = (bf16[12,2,64,256]{3,2,1,0:T(8,128)(2,1)S(1)}, bf16[12,2,64,256]{3,2,1,0:T(8,128)(2,1)S(1)}, u32[]{:S(2)}, u32[]{:S(2)}) collective-permute-start(bf16[12,2,64,256]{3,2,1,0:T(8,128)(2,1)S(1)} %get-tuple-element.10.refs_0_), channel_id=1, source_target_pairs={{0,2},{2,4},{4,6},{6,7},{7,5},{5,3},{3,1},{1,0},{8,10},{10,12},{12... | collective-permute-start | bytes 2359304 | tf_op jit(solution)/shard_map/ppermute | solution.py:248
  5.4 2.0 %collective-permute-start.16 = (bf16[12,2,64,256]{3,2,1,0:T(8,128)(2,1)S(1)}, bf16[12,2,64,256]{3,2,1,0:T(8,128)(2,1)}, u32[]{:S(2)}, u32[]{:S(2)}) collective-permute-start(bf16[12,2,64,256]{3,2,1,0:T(8,128)(2,1)S(1)} %get-tuple-element.11.refs_1_), channel_id=1, source_target_pairs={{0,2},{2,4},{4,6},{6,7},{7,5},{5,3},{3,1},{1,0},{8,10},{10,12},{12... | collective-permute-start | bytes 2359304 | tf_op jit(solution)/shard_map/ppermute | solution.py:248
  7.5 0.1 collective-permute-start.19
  7.6 16.2 %collective-permute-done.refs_4_ = bf16[12,2,64,256]{3,2,1,0:T(8,128)(2,1)S(1)} collective-permute-done((bf16[12,2,64,256]{3,2,1,0:T(8,128)(2,1)S(1)}, bf16[12,2,64,256]{3,2,1,0:T(8,128)(2,1)S(1)}, u32[]{:S(2)}, u32[]{:S(2)}) %collective-permute-start) | collective-permute-done | bytes 786464 | tf_op jit(solution)/shard_map/ppermute | solution.py:248
  23.8 2.1 %collective-permute-done.4.refs_5_ = bf16[12,2,64,256]{3,2,1,0:T(8,128)(2,1)S(1)} collective-permute-done((bf16[12,2,64,256]{3,2,1,0:T(8,128)(2,1)S(1)}, bf16[12,2,64,256]{3,2,1,0:T(8,128)(2,1)S(1)}, u32[]{:S(2)}, u32[]{:S(2)}) %collective-permute-start.4) | collective-permute-done | bytes 786464 | tf_op jit(solution)/shard_map/ppermute | solution.py:248
  25.8 14.6 %collective-permute-done.16.refs_4_ = bf16[12,2,64,256]{3,2,1,0:T(8,128)(2,1)} collective-permute-done((bf16[12,2,64,256]{3,2,1,0:T(8,128)(2,1)S(1)}, bf16[12,2,64,256]{3,2,1,0:T(8,128)(2,1)}, u32[]{:S(2)}, u32[]{:S(2)}) %collective-permute-start.16) | collective-permute-done | bytes 786464 | tf_op jit(solution)/shard_map/ppermute | solution.py:248
  40.5 1.8 %collective-permute-start.1 = (bf16[12,2,64,256]{3,2,1,0:T(8,128)(2,1)S(1)}, bf16[12,2,64,256]{3,2,1,0:T(8,128)(2,1)}, u32[]{:S(2)}, u32[]{:S(2)}) collective-permute-start(bf16[12,2,64,256]{3,2,1,0:T(8,128)(2,1)S(1)} %collective-permute-done.refs_4_), channel_id=1, source_target_pairs={{0,2},{2,4},{4,6},{6,7},{7,5},{5,3},{3,1},{1,0},{8,10},{10,12},{12... | collective-permute-start | bytes 2359304 | tf_op jit(solution)/shard_map/ppermute | solution.py:248
  42.3 0.9 copy-done.2
  43.2 0.2 collective-permute-start.5
  43.4 0.9 copy-done.4
  44.4 0.9 copy-done.6
  45.2 0.9 copy-done.8
  46.1 1.8 %collective-permute-start.17 = (bf16[12,2,64,256]{3,2,1,0:T(8,128)(2,1)}, bf16[12,2,64,256]{3,2,1,0:T(8,128)(2,1)}, u32[]{:S(2)}, u32[]{:S(2)}) collective-permute-start(bf16[12,2,64,256]{3,2,1,0:T(8,128)(2,1)} %collective-permute-done.16.refs_4_), channel_id=1, source_target_pairs={{0,2},{2,4},{4,6},{6,7},{7,5},{5,3},{3,1},{1,0},{8,10},{10,12},{12... | collective-permute-start | bytes 2359304 | tf_op jit(solution)/shard_map/ppermute | solution.py:248
  47.9 0.9 copy-done.10
  48.8 0.2 collective-permute-start.20
  49.1 11.9 %collective-permute-done.1.refs_4_ = bf16[12,2,64,256]{3,2,1,0:T(8,128)(2,1)} collective-permute-done((bf16[12,2,64,256]{3,2,1,0:T(8,128)(2,1)S(1)}, bf16[12,2,64,256]{3,2,1,0:T(8,128)(2,1)}, u32[]{:S(2)}, u32[]{:S(2)}) %collective-permute-start.1) | collective-permute-done | bytes 786464 | tf_op jit(solution)/shard_map/ppermute | solution.py:248
  61.0 2.7 %collective-permute-done.5.refs_5_ = bf16[12,2,64,256]{3,2,1,0:T(8,128)(2,1)} collective-permute-done((bf16[12,2,64,256]{3,2,1,0:T(8,128)(2,1)S(1)}, bf16[12,2,64,256]{3,2,1,0:T(8,128)(2,1)}, u32[]{:S(2)}, u32[]{:S(2)}) %collective-permute-start.5) | collective-permute-done | bytes 786464 | tf_op jit(solution)/shard_map/ppermute | solution.py:248
  63.7 0.9 copy-done.12
  64.6 1.6 collective-permute-start.2
  66.2 0.8 pad_add_fusion
  67.0 0.1 dynamic_slice.10
  67.1 1.2 dynamic_slice.12
  68.3 0.6 fusion.1
  68.9 8.9 %collective-permute-done.17.refs_4_ = bf16[12,2,64,256]{3,2,1,0:T(8,128)(2,1)} collective-permute-done((bf16[12,2,64,256]{3,2,1,0:T(8,128)(2,1)}, bf16[12,2,64,256]{3,2,1,0:T(8,128)(2,1)}, u32[]{:S(2)}, u32[]{:S(2)}) %collective-permute-start.17) | collective-permute-done | bytes 786464 | tf_op jit(solution)/shard_map/ppermute | solution.py:248
  77.9 1.7 %collective-permute-start.6 = (bf16[12,2,64,256]{3,2,1,0:T(8,128)(2,1)}, bf16[12,2,64,256]{3,2,1,0:T(8,128)(2,1)}, u32[]{:S(2)}, u32[]{:S(2)}) collective-permute-start(bf16[12,2,64,256]{3,2,1,0:T(8,128)(2,1)} %collective-permute-done.5.refs_5_), channel_id=1, source_target_pairs={{2,0},{4,2},{6,4},{7,6},{5,7},{3,5},{1,3},{0,1},{10,8},{12,10},{14... | collective-permute-start | bytes 2359304 | tf_op jit(solution)/shard_map/ppermute | solution.py:248
  79.7 0.2 collective-permute-done.20.refs_5_
  79.8 0.5 collective-permute-start.27
  80.3 1.3 gather_fusion
  81.7 1.6 collective-permute-start.18
  83.3 11.4 %collective-permute-done.2.refs_4_ = bf16[12,2,64,256]{3,2,1,0:T(8,128)(2,1)} collective-permute-done((bf16[12,2,64,256]{3,2,1,0:T(8,128)(2,1)}, bf16[12,2,64,256]{3,2,1,0:T(8,128)(2,1)}, u32[]{:S(2)}, u32[]{:S(2)}) %collective-permute-start.2) | collective-permute-done | bytes 786464 | tf_op jit(solution)/shard_map/ppermute | solution.py:248
  94.7 1.7 %collective-permute-start.21 = (bf16[12,2,64,256]{3,2,1,0:T(8,128)(2,1)}, bf16[12,2,64,256]{3,2,1,0:T(8,128)(2,1)}, u32[]{:S(2)}, u32[]{:S(2)}) collective-permute-start(bf16[12,2,64,256]{3,2,1,0:T(8,128)(2,1)} %collective-permute-done.20.refs_5_), channel_id=1, source_target_pairs={{2,0},{4,2},{6,4},{7,6},{5,7},{3,5},{1,3},{0,1},{10,8},{12,10},{14... | collective-permute-start | bytes 2359304 | tf_op jit(solution)/shard_map/ppermute | solution.py:248
  96.5 2.1 %fusion.4 = (bf16[12,2,32,256]{3,2,1,0:T(8,128)(2,1)}, bf16[12,2,32,256]{3,2,1,0:T(8,128)(2,1)}) fusion(bf16[12,2,64,256]{3,2,1,0:T(8,128)(2,1)} %collective-permute-done.2.refs_4_), kind=kLoop, calls=%fused_computation.17 | loop fusion | bytes 1572864 | tf_op jit(solution)/shard_map/slice | solution.py:247
  98.5 0.3 collective-permute-start.12
  98.8 2.1 %fusion.3 = (bf16[12,2,32,256]{3,2,1,0:T(8,128)(2,1)}, bf16[12,2,32,256]{3,2,1,0:T(8,128)(2,1)}) fusion(bf16[12,2,64,256]{3,2,1,0:T(8,128)(2,1)} %collective-permute-done.6.refs_5_), kind=kLoop, calls=%fused_computation.16 | loop fusion | bytes 1572864 | tf_op jit(solution)/shard_map/slice | solution.py:247
  100.9 1.7 %collective-permute-start.13 = (bf16[12,2,32,256]{3,2,1,0:T(8,128)(2,1)}, bf16[12,2,32,256]{3,2,1,0:T(8,128)(2,1)}, u32[]{:S(2)}, u32[]{:S(2)}) collective-permute-start(bf16[12,2,32,256]{3,2,1,0:T(8,128)(2,1)} %get-tuple-element.15), channel_id=1, source_target_pairs={{2,0},{4,2},{6,4},{7,6},{5,7},{3,5},{1,3},{0,1},{10,8},{12,10},{14... | collective-permute-start | bytes 1179656 | tf_op jit(solution)/shard_map/ppermute | solution.py:248
  102.6 0.3 collective-permute-start.3
  102.9 8.6 %collective-permute-done.18.refs_4_ = bf16[12,2,64,256]{3,2,1,0:T(8,128)(2,1)} collective-permute-done((bf16[12,2,64,256]{3,2,1,0:T(8,128)(2,1)}, bf16[12,2,64,256]{3,2,1,0:T(8,128)(2,1)}, u32[]{:S(2)}, u32[]{:S(2)}) %collective-permute-start.18) | collective-permute-done | bytes 786464 | tf_op jit(solution)/shard_map/ppermute | solution.py:248
  111.6 0.1 dynamic-slice_bitcast_fusion
  111.6 0.1 add.109
  111.7 0.1 copy.36.own_vir
  111.8 0.6 gather_fusion.1
  112.4 7.2 %gather_fusion.2 = s32[1152]{0:T(1024)S(1)} fusion(s32[16,128]{1,0:T(8,128)S(1)} %gather_fusion.1, s32[1152]{0:T(1024)S(1)} %copy-done.14), kind=kCustom, calls=%fused_computation.2 | custom fusion | bytes 18432 | tf_op jit(solution)/shard_map/gather | solution.py:265
  119.6 0.6 collective-permute-start.25
  120.2 0.1 collective-permute-start.22
  120.3 0.1 broadcast_in_dim.10.occ_pairs
  120.4 3.4 %shard_map.91.refs_8_ = f32[2,128,3072]{2,1,0:T(8,128)S(1)} custom-call(s32[8,1,128]{2,1,0:T(1,128)S(1)} %broadcast_in_dim.10.occ_pairs, s32[128,1]{1,0:T(8,128)S(1)} %copy.36.own_vir, s32[9,1,128]{2,1,0:T(1,128)S(1)} %broadcast_in_dim.25.vir_rows, bf16[12,2,64,256]{3,2,1,0:T(8,128)(2,1)S(1)} %get-tuple-element.10.refs_0_, ...), custom_call_target="tpu_custom_call" | custom-call | flops 2013265920 | bytes 12582912 | tf_op jit(solution)/shard_map/pallas_call | solution.py:204
  123.9 2.0 %collective-permute-start.7 = (bf16[12,2,32,256]{3,2,1,0:T(8,128)(2,1)S(1)}, bf16[12,2,32,256]{3,2,1,0:T(8,128)(2,1)S(1)}, u32[]{:S(2)}, u32[]{:S(2)}) collective-permute-start(bf16[12,2,32,256]{3,2,1,0:T(8,128)(2,1)S(1)} %copy-done.15), channel_id=1, source_target_pairs={{2,0},{4,2},{6,4},{7,6},{5,7},{3,5},{1,3},{0,1},{10,8},{12,10},{14... | collective-permute-start | bytes 1179656 | tf_op jit(solution)/shard_map/ppermute | solution.py:248
  125.9 2.1 %collective-permute-done.3.refs_4_.refs_2_ = bf16[12,2,32,256]{3,2,1,0:T(8,128)(2,1)} collective-permute-done((bf16[12,2,32,256]{3,2,1,0:T(8,128)(2,1)}, bf16[12,2,32,256]{3,2,1,0:T(8,128)(2,1)}, u32[]{:S(2)}, u32[]{:S(2)}) %collective-permute-start.3) | collective-permute-done | bytes 393248 | tf_op jit(solution)/shard_map/ppermute | solution.py:248
  128.0 3.7 %shard_map.92.refs_8_ = f32[2,128,3072]{2,1,0:T(8,128)S(1)} custom-call(s32[8,1,128]{2,1,0:T(1,128)S(1)} %broadcast_in_dim.10.occ_pairs, s32[128,1]{1,0:T(8,128)S(1)} %copy.36.own_vir, s32[9,1,128]{2,1,0:T(1,128)S(1)} %broadcast_in_dim.25.vir_rows, bf16[12,2,64,256]{3,2,1,0:T(8,128)(2,1)S(1)} %get-tuple-element.10.refs_0_, ...), custom_call_target="tpu_custom_call", output_to_operand_aliasing={{}: (11, {})} | custom-call | flops 2013265920 | bytes 12582912 | tf_op jit(solution)/shard_map/pallas_call | solution.py:204
  131.7 5.1 %shard_map.93.refs_8_ = f32[2,128,3072]{2,1,0:T(8,128)S(1)} custom-call(s32[8,1,128]{2,1,0:T(1,128)S(1)} %broadcast_in_dim.10.occ_pairs, s32[128,1]{1,0:T(8,128)S(1)} %copy.36.own_vir, s32[9,1,128]{2,1,0:T(1,128)S(1)} %broadcast_in_dim.25.vir_rows, bf16[12,2,64,256]{3,2,1,0:T(8,128)(2,1)S(1)} %get-tuple-element.10.refs_0_, ...), custom_call_target="tpu_custom_call", output_to_operand_aliasing={{}: (11, {})} | custom-call | flops 2013265920 | bytes 12582912 | tf_op jit(solution)/shard_map/pallas_call | solution.py:204
  136.8 5.6 %shard_map.94.refs_8_ = f32[2,128,3072]{2,1,0:T(8,128)S(1)} custom-call(s32[8,1,128]{2,1,0:T(1,128)S(1)} %broadcast_in_dim.10.occ_pairs, s32[128,1]{1,0:T(8,128)S(1)} %copy.36.own_vir, s32[9,1,128]{2,1,0:T(1,128)S(1)} %broadcast_in_dim.25.vir_rows, bf16[12,2,64,256]{3,2,1,0:T(8,128)(2,1)S(1)} %get-tuple-element.10.refs_0_, ...), custom_call_target="tpu_custom_call", output_to_operand_aliasing={{}: (11, {})} | custom-call | flops 2013265920 | bytes 12582912 | tf_op jit(solution)/shard_map/pallas_call | solution.py:204
  142.4 0.6 collective-permute-start.14
  143.0 0.1 collective-permute-start.15
  143.0 5.5 %shard_map.95.refs_8_ = f32[2,128,3072]{2,1,0:T(8,128)S(1)} custom-call(s32[8,1,128]{2,1,0:T(1,128)S(1)} %broadcast_in_dim.10.occ_pairs, s32[128,1]{1,0:T(8,128)S(1)} %copy.36.own_vir, s32[9,1,128]{2,1,0:T(1,128)S(1)} %broadcast_in_dim.25.vir_rows, bf16[12,2,64,256]{3,2,1,0:T(8,128)(2,1)S(1)} %get-tuple-element.10.refs_0_, ...), custom_call_target="tpu_custom_call", output_to_operand_aliasing={{}: (11, {})} | custom-call | flops 2013265920 | bytes 12582912 | tf_op jit(solution)/shard_map/pallas_call | solution.py:204
  148.6 0.5 collective-permute-start.8
  149.1 0.1 collective-permute-start.9
  149.2 5.3 %shard_map.96.refs_8_ = f32[2,128,3072]{2,1,0:T(8,128)S(1)} custom-call(s32[8,1,128]{2,1,0:T(1,128)S(1)} %broadcast_in_dim.10.occ_pairs, s32[128,1]{1,0:T(8,128)S(1)} %copy.36.own_vir, s32[9,1,128]{2,1,0:T(1,128)S(1)} %broadcast_in_dim.25.vir_rows, bf16[12,2,64,256]{3,2,1,0:T(8,128)(2,1)S(1)} %get-tuple-element.10.refs_0_, ...), custom_call_target="tpu_custom_call", output_to_operand_aliasing={{}: (11, {})} | custom-call | flops 2013265920 | bytes 12582912 | tf_op jit(solution)/shard_map/pallas_call | solution.py:204
  154.5 5.1 %shard_map.97.refs_8_ = f32[2,128,3072]{2,1,0:T(8,128)S(1)} custom-call(s32[8,1,128]{2,1,0:T(1,128)S(1)} %broadcast_in_dim.10.occ_pairs, s32[128,1]{1,0:T(8,128)S(1)} %copy.36.own_vir, s32[9,1,128]{2,1,0:T(1,128)S(1)} %broadcast_in_dim.25.vir_rows, bf16[12,2,64,256]{3,2,1,0:T(8,128)(2,1)S(1)} %get-tuple-element.10.refs_0_, ...), custom_call_target="tpu_custom_call", output_to_operand_aliasing={{}: (11, {})} | custom-call | flops 2013265920 | bytes 12582912 | tf_op jit(solution)/shard_map/pallas_call | solution.py:204
  159.6 4.6 %shard_map.98.refs_6_ = f32[2,128,3072]{2,1,0:T(8,128)S(1)} custom-call(s32[8,1,128]{2,1,0:T(1,128)S(1)} %broadcast_in_dim.10.occ_pairs, s32[128,1]{1,0:T(8,128)S(1)} %copy.36.own_vir, s32[9,1,128]{2,1,0:T(1,128)S(1)} %broadcast_in_dim.25.vir_rows, bf16[12,2,64,256]{3,2,1,0:T(8,128)(2,1)S(1)} %get-tuple-element.10.refs_0_, ...), custom_call_target="tpu_custom_call", output_to_operand_aliasing={{}: (11, {})} | custom-call | flops 1006632960 | bytes 11010048 | tf_op jit(solution)/shard_map/pallas_call | solution.py:204
  164.3 2.4 %shard_map.99 = (bf16[256,128]{1,0:T(8,128)(2,1)S(1)}, bf16[256,128]{1,0:T(8,128)(2,1)S(1)}, f32[2,128,3072]{2,1,0:T(8,128)S(1)}) custom-call(s32[8,1,128]{2,1,0:T(1,128)S(1)} %broadcast_in_dim.10.occ_pairs, s32[128,1]{1,0:T(8,128)S(1)} %copy.36.own_vir, s32[9,1,128]{2,1,0:T(1,128)S(1)} %broadcast_in_dim.25.vir_rows, ...), custom_call_target="tpu_custom_call" | custom-call | flops 402653184 | bytes 11010048 | tf_op jit(solution)/shard_map/pallas_call | solution.py:204
  166.7 3.9 %shard_map.100 = f32[2,128,3072]{2,1,0:T(8,128)} custom-call(s32[8,1,128]{2,1,0:T(1,128)S(1)} %broadcast_in_dim.10.occ_pairs, s32[128,1]{1,0:T(8,128)S(1)} %copy.36.own_vir, s32[9,1,128]{2,1,0:T(1,128)S(1)} %broadcast_in_dim.25.vir_rows, bf16[12,2,64,256]{3,2,1,0:T(8,128)(2,1)S(1)} %get-tuple-element.10.refs_0_, ...), custom_call_target="tpu_custom_call" | custom-call | flops 603979776 | bytes 11010048 | tf_op jit(solution)/shard_map/pallas_call | solution.py:204
  (65 shorter events, 0.2 us)
Async XLA Ops:
  0.0 111.6 %copy-start = (s32[1024]{0:T(1024)S(1)}, s32[1024]{0:T(1024)}, u32[]{:S(2)}) copy-start(s32[1024]{0:T(1024)} %param.11) | copy-start | bytes 12292
  0.0 1.4 copy-start.1
  1.4 111.0 %copy-start.14 = (s32[1152]{0:T(1024)S(1)}, s32[1152]{0:T(1024)}, u32[]{:S(2)}) copy-start(s32[1152]{0:T(1024)} %constant.98) | copy-start | bytes 13828
  2.2 5.2 %collective-permute-start.10 = (bf16[12,2,64,256]{3,2,1,0:T(8,128)(2,1)S(1)}, bf16[12,2,64,256]{3,2,1,0:T(8,128)(2,1)S(1)}, u32[]{:S(2)}, u32[]{:S(2)}) collective-permute-start(bf16[12,2,64,256]{3,2,1,0:T(8,128)(2,1)S(1)} %get-tuple-element.10.refs_0_), channel_id=1, source_target_pairs={{8,0},{0,8},{9,1},{1,9},{10,2},{2,10},{11,3},{3,11},{12,4},{4,12},... | collective-permute-start | bytes 2359304 | tf_op jit(solution)/shard_map/ppermute | solution.py:235
  2.8 21.0 %collective-permute-start = (bf16[12,2,64,256]{3,2,1,0:T(8,128)(2,1)S(1)}, bf16[12,2,64,256]{3,2,1,0:T(8,128)(2,1)S(1)}, u32[]{:S(2)}, u32[]{:S(2)}) collective-permute-start(bf16[12,2,64,256]{3,2,1,0:T(8,128)(2,1)S(1)} %get-tuple-element.10.refs_0_), channel_id=1, source_target_pairs={{0,2},{2,4},{4,6},{6,7},{7,5},{5,3},{3,1},{1,0},{8,10},{10,12},{12... | collective-permute-start | bytes 2359304 | tf_op jit(solution)/shard_map/ppermute | solution.py:248
  5.4 20.4 %collective-permute-start.4 = (bf16[12,2,64,256]{3,2,1,0:T(8,128)(2,1)S(1)}, bf16[12,2,64,256]{3,2,1,0:T(8,128)(2,1)S(1)}, u32[]{:S(2)}, u32[]{:S(2)}) collective-permute-start(bf16[12,2,64,256]{3,2,1,0:T(8,128)(2,1)S(1)} %get-tuple-element.11.refs_1_), channel_id=1, source_target_pairs={{2,0},{4,2},{6,4},{7,6},{5,7},{3,5},{1,3},{0,1},{10,8},{12,10},{14... | collective-permute-start | bytes 2359304 | tf_op jit(solution)/shard_map/ppermute | solution.py:248
  5.4 35.0 %collective-permute-start.16 = (bf16[12,2,64,256]{3,2,1,0:T(8,128)(2,1)S(1)}, bf16[12,2,64,256]{3,2,1,0:T(8,128)(2,1)}, u32[]{:S(2)}, u32[]{:S(2)}) collective-permute-start(bf16[12,2,64,256]{3,2,1,0:T(8,128)(2,1)S(1)} %get-tuple-element.11.refs_1_), channel_id=1, source_target_pairs={{0,2},{2,4},{4,6},{6,7},{7,5},{5,3},{3,1},{1,0},{8,10},{10,12},{12... | collective-permute-start | bytes 2359304 | tf_op jit(solution)/shard_map/ppermute | solution.py:248
  7.4 33.0 %collective-permute-start.11 = (bf16[12,2,64,256]{3,2,1,0:T(8,128)(2,1)S(1)}, bf16[12,2,64,256]{3,2,1,0:T(8,128)(2,1)S(1)}, u32[]{:S(2)}, u32[]{:S(2)}) collective-permute-start(bf16[12,2,64,256]{3,2,1,0:T(8,128)(2,1)S(1)} %get-tuple-element.11.refs_1_), channel_id=1, source_target_pairs={{8,0},{0,8},{9,1},{1,9},{10,2},{2,10},{11,3},{3,11},{12,4},{4,12},... | collective-permute-start | bytes 2359304 | tf_op jit(solution)/shard_map/ppermute | solution.py:235
  7.5 35.7 %collective-permute-start.19 = (bf16[12,2,64,256]{3,2,1,0:T(8,128)(2,1)S(1)}, bf16[12,2,64,256]{3,2,1,0:T(8,128)(2,1)}, u32[]{:S(2)}, u32[]{:S(2)}) collective-permute-start(bf16[12,2,64,256]{3,2,1,0:T(8,128)(2,1)S(1)} %get-tuple-element.10.refs_0_), channel_id=1, source_target_pairs={{2,0},{4,2},{6,4},{7,6},{5,7},{3,5},{1,3},{0,1},{10,8},{12,10},{14... | collective-permute-start | bytes 2359304 | tf_op jit(solution)/shard_map/ppermute | solution.py:248
  23.8 20.6 %collective-permute-start.32 = (bf16[12,2,64,256]{3,2,1,0:T(8,128)(2,1)S(1)}, bf16[12,2,64,256]{3,2,1,0:T(8,128)(2,1)S(1)}, u32[]{:S(2)}, u32[]{:S(2)}) collective-permute-start(bf16[12,2,64,256]{3,2,1,0:T(8,128)(2,1)S(1)} %collective-permute-done.refs_4_), channel_id=1, source_target_pairs={{8,0},{0,8},{9,1},{1,9},{10,2},{2,10},{11,3},{3,11},{12,4},{4,12},... | collective-permute-start | bytes 2359304 | tf_op jit(solution)/shard_map/ppermute | solution.py:253
  25.8 19.4 %collective-permute-start.33 = (bf16[12,2,64,256]{3,2,1,0:T(8,128)(2,1)S(1)}, bf16[12,2,64,256]{3,2,1,0:T(8,128)(2,1)S(1)}, u32[]{:S(2)}, u32[]{:S(2)}) collective-permute-start(bf16[12,2,64,256]{3,2,1,0:T(8,128)(2,1)S(1)} %collective-permute-done.4.refs_5_), channel_id=1, source_target_pairs={{8,0},{0,8},{9,1},{1,9},{10,2},{2,10},{11,3},{3,11},{12,4},{4,12},... | collective-permute-start | bytes 2359304 | tf_op jit(solution)/shard_map/ppermute | solution.py:253
  40.5 7.5 %collective-permute-start.30 = (bf16[12,2,64,256]{3,2,1,0:T(8,128)(2,1)}, bf16[12,2,64,256]{3,2,1,0:T(8,128)(2,1)S(1)}, u32[]{:S(2)}, u32[]{:S(2)}) collective-permute-start(bf16[12,2,64,256]{3,2,1,0:T(8,128)(2,1)} %collective-permute-done.16.refs_4_), channel_id=1, source_target_pairs={{8,0},{0,8},{9,1},{1,9},{10,2},{2,10},{11,3},{3,11},{12,4},{4,12},... | collective-permute-start | bytes 2359304 | tf_op jit(solution)/shard_map/ppermute | solution.py:253
  40.5 20.5 %collective-permute-start.1 = (bf16[12,2,64,256]{3,2,1,0:T(8,128)(2,1)S(1)}, bf16[12,2,64,256]{3,2,1,0:T(8,128)(2,1)}, u32[]{:S(2)}, u32[]{:S(2)}) collective-permute-start(bf16[12,2,64,256]{3,2,1,0:T(8,128)(2,1)S(1)} %collective-permute-done.refs_4_), channel_id=1, source_target_pairs={{0,2},{2,4},{4,6},{6,7},{7,5},{5,3},{3,1},{1,0},{8,10},{10,12},{12... | collective-permute-start | bytes 2359304 | tf_op jit(solution)/shard_map/ppermute | solution.py:248
  42.3 0.9 copy-start.2
  43.2 20.5 %collective-permute-start.5 = (bf16[12,2,64,256]{3,2,1,0:T(8,128)(2,1)S(1)}, bf16[12,2,64,256]{3,2,1,0:T(8,128)(2,1)}, u32[]{:S(2)}, u32[]{:S(2)}) collective-permute-start(bf16[12,2,64,256]{3,2,1,0:T(8,128)(2,1)S(1)} %collective-permute-done.4.refs_5_), channel_id=1, source_target_pairs={{2,0},{4,2},{6,4},{7,6},{5,7},{3,5},{1,3},{0,1},{10,8},{12,10},{14... | collective-permute-start | bytes 2359304 | tf_op jit(solution)/shard_map/ppermute | solution.py:248
  43.4 0.9 copy-start.4
  44.4 0.9 copy-start.6
  45.2 18.5 %collective-permute-start.31 = (bf16[12,2,64,256]{3,2,1,0:T(8,128)(2,1)}, bf16[12,2,64,256]{3,2,1,0:T(8,128)(2,1)S(1)}, u32[]{:S(2)}, u32[]{:S(2)}) collective-permute-start(bf16[12,2,64,256]{3,2,1,0:T(8,128)(2,1)} %collective-permute-done.19.refs_5_), channel_id=1, source_target_pairs={{8,0},{0,8},{9,1},{1,9},{10,2},{2,10},{11,3},{3,11},{12,4},{4,12},... | collective-permute-start | bytes 2359304 | tf_op jit(solution)/shard_map/ppermute | solution.py:253
  45.2 0.9 copy-start.8
  46.1 31.7 %collective-permute-start.17 = (bf16[12,2,64,256]{3,2,1,0:T(8,128)(2,1)}, bf16[12,2,64,256]{3,2,1,0:T(8,128)(2,1)}, u32[]{:S(2)}, u32[]{:S(2)}) collective-permute-start(bf16[12,2,64,256]{3,2,1,0:T(8,128)(2,1)} %collective-permute-done.16.refs_4_), channel_id=1, source_target_pairs={{0,2},{2,4},{4,6},{6,7},{7,5},{5,3},{3,1},{1,0},{8,10},{10,12},{12... | collective-permute-start | bytes 2359304 | tf_op jit(solution)/shard_map/ppermute | solution.py:248
  47.9 0.9 copy-start.10
  48.8 31.0 %collective-permute-start.20 = (bf16[12,2,64,256]{3,2,1,0:T(8,128)(2,1)}, bf16[12,2,64,256]{3,2,1,0:T(8,128)(2,1)}, u32[]{:S(2)}, u32[]{:S(2)}) collective-permute-start(bf16[12,2,64,256]{3,2,1,0:T(8,128)(2,1)} %collective-permute-done.19.refs_5_), channel_id=1, source_target_pairs={{2,0},{4,2},{6,4},{7,6},{5,7},{3,5},{1,3},{0,1},{10,8},{12,10},{14... | collective-permute-start | bytes 2359304 | tf_op jit(solution)/shard_map/ppermute | solution.py:248
  61.0 18.8 %collective-permute-start.28 = (bf16[12,2,64,256]{3,2,1,0:T(8,128)(2,1)}, bf16[12,2,64,256]{3,2,1,0:T(8,128)(2,1)}, u32[]{:S(2)}, u32[]{:S(2)}) collective-permute-start(bf16[12,2,64,256]{3,2,1,0:T(8,128)(2,1)} %collective-permute-done.1.refs_4_), channel_id=1, source_target_pairs={{8,0},{0,8},{9,1},{1,9},{10,2},{2,10},{11,3},{3,11},{12,4},{4,12},... | collective-permute-start | bytes 2359304 | tf_op jit(solution)/shard_map/ppermute | solution.py:253
  63.7 17.9 %collective-permute-start.29 = (bf16[12,2,64,256]{3,2,1,0:T(8,128)(2,1)}, bf16[12,2,64,256]{3,2,1,0:T(8,128)(2,1)}, u32[]{:S(2)}, u32[]{:S(2)}) collective-permute-start(bf16[12,2,64,256]{3,2,1,0:T(8,128)(2,1)} %collective-permute-done.5.refs_5_), channel_id=1, source_target_pairs={{8,0},{0,8},{9,1},{1,9},{10,2},{2,10},{11,3},{3,11},{12,4},{4,12},... | collective-permute-start | bytes 2359304 | tf_op jit(solution)/shard_map/ppermute | solution.py:253
  63.7 0.9 copy-start.12
  64.6 30.1 %collective-permute-start.2 = (bf16[12,2,64,256]{3,2,1,0:T(8,128)(2,1)}, bf16[12,2,64,256]{3,2,1,0:T(8,128)(2,1)}, u32[]{:S(2)}, u32[]{:S(2)}) collective-permute-start(bf16[12,2,64,256]{3,2,1,0:T(8,128)(2,1)} %collective-permute-done.1.refs_4_), channel_id=1, source_target_pairs={{0,2},{2,4},{4,6},{6,7},{7,5},{5,3},{3,1},{1,0},{8,10},{10,12},{12... | collective-permute-start | bytes 2359304 | tf_op jit(solution)/shard_map/ppermute | solution.py:248
  77.9 20.7 %collective-permute-start.6 = (bf16[12,2,64,256]{3,2,1,0:T(8,128)(2,1)}, bf16[12,2,64,256]{3,2,1,0:T(8,128)(2,1)}, u32[]{:S(2)}, u32[]{:S(2)}) collective-permute-start(bf16[12,2,64,256]{3,2,1,0:T(8,128)(2,1)} %collective-permute-done.5.refs_5_), channel_id=1, source_target_pairs={{2,0},{4,2},{6,4},{7,6},{5,7},{3,5},{1,3},{0,1},{10,8},{12,10},{14... | collective-permute-start | bytes 2359304 | tf_op jit(solution)/shard_map/ppermute | solution.py:248
  79.8 21.1 %collective-permute-start.26 = (bf16[12,2,64,256]{3,2,1,0:T(8,128)(2,1)}, bf16[12,2,64,256]{3,2,1,0:T(8,128)(2,1)}, u32[]{:S(2)}, u32[]{:S(2)}) collective-permute-start(bf16[12,2,64,256]{3,2,1,0:T(8,128)(2,1)} %collective-permute-done.17.refs_4_), channel_id=1, source_target_pairs={{8,0},{0,8},{9,1},{1,9},{10,2},{2,10},{11,3},{3,11},{12,4},{4,12},... | collective-permute-start | bytes 2359304 | tf_op jit(solution)/shard_map/ppermute | solution.py:253
  79.8 22.8 %collective-permute-start.27 = (bf16[12,2,64,256]{3,2,1,0:T(8,128)(2,1)}, bf16[12,2,64,256]{3,2,1,0:T(8,128)(2,1)}, u32[]{:S(2)}, u32[]{:S(2)}) collective-permute-start(bf16[12,2,64,256]{3,2,1,0:T(8,128)(2,1)} %collective-permute-done.20.refs_5_), channel_id=1, source_target_pairs={{8,0},{0,8},{9,1},{1,9},{10,2},{2,10},{11,3},{3,11},{12,4},{4,12},... | collective-permute-start | bytes 2359304 | tf_op jit(solution)/shard_map/ppermute | solution.py:253
  81.7 29.9 %collective-permute-start.18 = (bf16[12,2,64,256]{3,2,1,0:T(8,128)(2,1)}, bf16[12,2,64,256]{3,2,1,0:T(8,128)(2,1)}, u32[]{:S(2)}, u32[]{:S(2)}) collective-permute-start(bf16[12,2,64,256]{3,2,1,0:T(8,128)(2,1)} %collective-permute-done.17.refs_4_), channel_id=1, source_target_pairs={{0,2},{2,4},{4,6},{6,7},{7,5},{5,3},{3,1},{1,0},{8,10},{10,12},{12... | collective-permute-start | bytes 2359304 | tf_op jit(solution)/shard_map/ppermute | solution.py:248
  94.7 24.9 %collective-permute-start.21 = (bf16[12,2,64,256]{3,2,1,0:T(8,128)(2,1)}, bf16[12,2,64,256]{3,2,1,0:T(8,128)(2,1)}, u32[]{:S(2)}, u32[]{:S(2)}) collective-permute-start(bf16[12,2,64,256]{3,2,1,0:T(8,128)(2,1)} %collective-permute-done.20.refs_5_), channel_id=1, source_target_pairs={{2,0},{4,2},{6,4},{7,6},{5,7},{3,5},{1,3},{0,1},{10,8},{12,10},{14... | collective-permute-start | bytes 2359304 | tf_op jit(solution)/shard_map/ppermute | solution.py:248
  98.5 21.7 %collective-permute-start.12 = (bf16[12,2,32,256]{3,2,1,0:T(8,128)(2,1)}, bf16[12,2,32,256]{3,2,1,0:T(8,128)(2,1)}, u32[]{:S(2)}, u32[]{:S(2)}) collective-permute-start(bf16[12,2,32,256]{3,2,1,0:T(8,128)(2,1)} %get-tuple-element.17), channel_id=1, source_target_pairs={{0,2},{2,4},{4,6},{6,7},{7,5},{5,3},{3,1},{1,0},{8,10},{10,12},{12... | collective-permute-start | bytes 1179656 | tf_op jit(solution)/shard_map/ppermute | solution.py:248
  100.9 22.9 %collective-permute-start.13 = (bf16[12,2,32,256]{3,2,1,0:T(8,128)(2,1)}, bf16[12,2,32,256]{3,2,1,0:T(8,128)(2,1)}, u32[]{:S(2)}, u32[]{:S(2)}) collective-permute-start(bf16[12,2,32,256]{3,2,1,0:T(8,128)(2,1)} %get-tuple-element.15), channel_id=1, source_target_pairs={{2,0},{4,2},{6,4},{7,6},{5,7},{3,5},{1,3},{0,1},{10,8},{12,10},{14... | collective-permute-start | bytes 1179656 | tf_op jit(solution)/shard_map/ppermute | solution.py:248
  102.6 25.3 %collective-permute-start.3 = (bf16[12,2,32,256]{3,2,1,0:T(8,128)(2,1)}, bf16[12,2,32,256]{3,2,1,0:T(8,128)(2,1)}, u32[]{:S(2)}, u32[]{:S(2)}) collective-permute-start(bf16[12,2,32,256]{3,2,1,0:T(8,128)(2,1)} %get-tuple-element.18), channel_id=1, source_target_pairs={{0,2},{2,4},{4,6},{6,7},{7,5},{5,3},{3,1},{1,0},{8,10},{10,12},{12... | collective-permute-start | bytes 1179656 | tf_op jit(solution)/shard_map/ppermute | solution.py:248
  111.6 31.4 %collective-permute-start.24 = (bf16[12,2,64,256]{3,2,1,0:T(8,128)(2,1)}, bf16[12,2,64,256]{3,2,1,0:T(8,128)(2,1)}, u32[]{:S(2)}, u32[]{:S(2)}) collective-permute-start(bf16[12,2,64,256]{3,2,1,0:T(8,128)(2,1)} %collective-permute-done.2.refs_4_), channel_id=1, source_target_pairs={{8,0},{0,8},{9,1},{1,9},{10,2},{2,10},{11,3},{3,11},{12,4},{4,12},... | collective-permute-start | bytes 2359304 | tf_op jit(solution)/shard_map/ppermute | solution.py:253
  119.6 29.0 %collective-permute-start.25 = (bf16[12,2,64,256]{3,2,1,0:T(8,128)(2,1)}, bf16[12,2,64,256]{3,2,1,0:T(8,128)(2,1)S(1)}, u32[]{:S(2)}, u32[]{:S(2)}) collective-permute-start(bf16[12,2,64,256]{3,2,1,0:T(8,128)(2,1)} %collective-permute-done.6.refs_5_), channel_id=1, source_target_pairs={{8,0},{0,8},{9,1},{1,9},{10,2},{2,10},{11,3},{3,11},{12,4},{4,12},... | collective-permute-start | bytes 2359304 | tf_op jit(solution)/shard_map/ppermute | solution.py:253
  120.2 28.9 %collective-permute-start.22 = (bf16[12,2,64,256]{3,2,1,0:T(8,128)(2,1)}, bf16[12,2,64,256]{3,2,1,0:T(8,128)(2,1)S(1)}, u32[]{:S(2)}, u32[]{:S(2)}) collective-permute-start(bf16[12,2,64,256]{3,2,1,0:T(8,128)(2,1)} %collective-permute-done.18.refs_4_), channel_id=1, source_target_pairs={{8,0},{0,8},{9,1},{1,9},{10,2},{2,10},{11,3},{3,11},{12,4},{4,12},... | collective-permute-start | bytes 2359304 | tf_op jit(solution)/shard_map/ppermute | solution.py:253
  120.4 3.5 %copy-start.15 = (bf16[12,2,32,256]{3,2,1,0:T(8,128)(2,1)S(1)}, bf16[12,2,32,256]{3,2,1,0:T(8,128)(2,1)}, u32[]{:S(2)}) copy-start(bf16[12,2,32,256]{3,2,1,0:T(8,128)(2,1)} %get-tuple-element.16) | copy-start | bytes 1179652
  120.4 7.6 %copy-start.3 = (bf16[12,2,64,256]{3,2,1,0:T(8,128)(2,1)S(1)}, bf16[12,2,64,256]{3,2,1,0:T(8,128)(2,1)}, u32[]{:S(2)}) copy-start(bf16[12,2,64,256]{3,2,1,0:T(8,128)(2,1)} %copy-done.2) | copy-start | bytes 2359300
  120.4 7.6 %copy-start.5 = (bf16[12,2,64,256]{3,2,1,0:T(8,128)(2,1)S(1)}, bf16[12,2,64,256]{3,2,1,0:T(8,128)(2,1)}, u32[]{:S(2)}) copy-start(bf16[12,2,64,256]{3,2,1,0:T(8,128)(2,1)} %copy-done.4) | copy-start | bytes 2359300
  120.4 7.6 %copy-start.7 = (bf16[12,2,64,256]{3,2,1,0:T(8,128)(2,1)S(1)}, bf16[12,2,64,256]{3,2,1,0:T(8,128)(2,1)}, u32[]{:S(2)}) copy-start(bf16[12,2,64,256]{3,2,1,0:T(8,128)(2,1)} %copy-done.6) | copy-start | bytes 2359300
  120.4 7.6 %copy-start.9 = (bf16[12,2,64,256]{3,2,1,0:T(8,128)(2,1)S(1)}, bf16[12,2,64,256]{3,2,1,0:T(8,128)(2,1)}, u32[]{:S(2)}) copy-start(bf16[12,2,64,256]{3,2,1,0:T(8,128)(2,1)} %copy-done.8) | copy-start | bytes 2359300
  123.9 7.8 %copy-start.11 = (bf16[12,2,64,256]{3,2,1,0:T(8,128)(2,1)S(1)}, bf16[12,2,64,256]{3,2,1,0:T(8,128)(2,1)}, u32[]{:S(2)}) copy-start(bf16[12,2,64,256]{3,2,1,0:T(8,128)(2,1)} %copy-done.10) | copy-start | bytes 2359300
  123.9 7.8 %copy-start.13 = (bf16[12,2,64,256]{3,2,1,0:T(8,128)(2,1)S(1)}, bf16[12,2,64,256]{3,2,1,0:T(8,128)(2,1)}, u32[]{:S(2)}) copy-start(bf16[12,2,64,256]{3,2,1,0:T(8,128)(2,1)} %copy-done.12) | copy-start | bytes 2359300
  123.9 18.5 %collective-permute-start.7 = (bf16[12,2,32,256]{3,2,1,0:T(8,128)(2,1)S(1)}, bf16[12,2,32,256]{3,2,1,0:T(8,128)(2,1)S(1)}, u32[]{:S(2)}, u32[]{:S(2)}) collective-permute-start(bf16[12,2,32,256]{3,2,1,0:T(8,128)(2,1)S(1)} %copy-done.15), channel_id=1, source_target_pairs={{2,0},{4,2},{6,4},{7,6},{5,7},{3,5},{1,3},{0,1},{10,8},{12,10},{14... | collective-permute-start | bytes 1179656 | tf_op jit(solution)/shard_map/ppermute | solution.py:248
  128.0 26.6 %collective-permute-start.23 = (bf16[12,2,64,256]{3,2,1,0:T(8,128)(2,1)}, bf16[12,2,64,256]{3,2,1,0:T(8,128)(2,1)S(1)}, u32[]{:S(2)}, u32[]{:S(2)}) collective-permute-start(bf16[12,2,64,256]{3,2,1,0:T(8,128)(2,1)} %collective-permute-done.21.refs_5_), channel_id=1, source_target_pairs={{8,0},{0,8},{9,1},{1,9},{10,2},{2,10},{11,3},{3,11},{12,4},{4,12},... | collective-permute-start | bytes 2359304 | tf_op jit(solution)/shard_map/ppermute | solution.py:253
  142.4 17.2 %collective-permute-start.14 = (bf16[12,2,32,256]{3,2,1,0:T(8,128)(2,1)}, bf16[12,2,32,256]{3,2,1,0:T(8,128)(2,1)S(1)}, u32[]{:S(2)}, u32[]{:S(2)}) collective-permute-start(bf16[12,2,32,256]{3,2,1,0:T(8,128)(2,1)} %collective-permute-done.12.refs_4_), channel_id=1, source_target_pairs={{8,0},{0,8},{9,1},{1,9},{10,2},{2,10},{11,3},{3,11},{12,4},{4,12},... | collective-permute-start | bytes 1179656 | tf_op jit(solution)/shard_map/ppermute | solution.py:253
  143.0 16.7 %collective-permute-start.15 = (bf16[12,2,32,256]{3,2,1,0:T(8,128)(2,1)}, bf16[12,2,32,256]{3,2,1,0:T(8,128)(2,1)S(1)}, u32[]{:S(2)}, u32[]{:S(2)}) collective-permute-start(bf16[12,2,32,256]{3,2,1,0:T(8,128)(2,1)} %collective-permute-done.13.refs_5_), channel_id=1, source_target_pairs={{8,0},{0,8},{9,1},{1,9},{10,2},{2,10},{11,3},{3,11},{12,4},{4,12},... | collective-permute-start | bytes 1179656 | tf_op jit(solution)/shard_map/ppermute | solution.py:253
  148.6 18.0 %collective-permute-start.8 = (bf16[12,2,32,256]{3,2,1,0:T(8,128)(2,1)}, bf16[12,2,32,256]{3,2,1,0:T(8,128)(2,1)S(1)}, u32[]{:S(2)}, u32[]{:S(2)}) collective-permute-start(bf16[12,2,32,256]{3,2,1,0:T(8,128)(2,1)} %collective-permute-done.3.refs_4_.refs_2_), channel_id=1, source_target_pairs={{8,0},{0,8},{9,1},{1,9},{10,2},{2,10},{11,3},{3,11},{12,4},{4,12},... | collective-permute-start | bytes 1179656 | tf_op jit(solution)/shard_map/ppermute | solution.py:253
  149.1 17.5 %collective-permute-start.9 = (bf16[12,2,32,256]{3,2,1,0:T(8,128)(2,1)S(1)}, bf16[12,2,32,256]{3,2,1,0:T(8,128)(2,1)S(1)}, u32[]{:S(2)}, u32[]{:S(2)}) collective-permute-start(bf16[12,2,32,256]{3,2,1,0:T(8,128)(2,1)S(1)} %collective-permute-done.7.refs_5_.refs_3_), channel_id=1, source_target_pairs={{8,0},{0,8},{9,1},{1,9},{10,2},{2,10},{11,3},{3,11},{12,4},{4,12},... | collective-permute-start | bytes 1179656 | tf_op jit(solution)/shard_map/ppermute | solution.py:253
where the time goes:
time: 171 us
  waiting for transfers between devices  78.8 us (46%)
  Pallas kernels  45.4 us (27%)
  starting transfers between devices  22.8 us (13%)
  local copies, waits for them, and re-layouts  21.8 us (13%)
    ppermute x16, waiting for transfers between devices, on_device(): held[way][step] = lax.ppermute(source, 'vir', links[way])  78.8 us
    pallas_call x10, Pallas kernels, block_step(): pl.pallas_call(functools.partial(block_kernel, layout), out_shape=out_sha...  44.6 us
    ppermute x16, starting transfers between devices, on_device(): held[way][step] = lax.ppermute(source, 'vir', links[way])  19.8 us
    gather x1, local copies, waits for them, and re-layouts, on_device(): vir_rows = energy_table[away + count, inner][:, None, :]  7.21 us
    unnamed x32, local copies, waits for them, and re-layouts  6.87 us
    slice x2, local copies, waits for them, and re-layouts, on_device(): lax.slice_in_dim(source, some * (step - at), some * (step - at + 1), axis=2)  4.15 us
  transfers between devices with their start and end apart: 34, of which 10 were waited for; matrix products, arithmetic and copies ran while one was open for 10% of the time, Pallas kernels for 24%

commit v1 on v0

--- a/solution.py
+++ b/solution.py
@@ -14,7 +14,7 @@
 last_cuts = 2
 body_steps = 2
 body_tiles = 3
-last_tiles = 6
+last_tiles = 3
 
 across = (((1,), (1,)), ((), ()))
 along = (((1,), (0,)), ((), ()))
@@ -70,27 +70,25 @@
 
 
 def block_kernel(layout, occ_pairs, own_vir, vir_rows, *refs):
-    number, parts, owned, count, steps, tiles, prior, stage = layout
+    number, parts, owned, count, steps, tiles, prior, place = layout
     refs = list(refs)
-    own = [[refs.pop(0) for _ in range(owned)] for _ in range(1 if stage == 2 else parts)]
-    if number:
-        groups = [[refs.pop(0) for _ in range(count)] for _ in range(1 if stage == 1 else parts)]
-    else:
-        groups = own
-    near_amplitude, near_swapped, held = (refs.pop(0) for _ in range(3)) if stage == 2 else (None, None, None)
-    density_in = refs.pop(0) if prior and stage != 2 else None
-    if stage == 1:
-        amplitude, swapped_out, density, direct, in_sem = refs
+    own = [[refs.pop(0) for _ in range(owned)] for _ in range(parts)]
+    groups = [[refs.pop(0) for _ in range(count)] for _ in range(parts)] if number else own
+    density_in = refs.pop(0) if prior else None
+    if place == "keep":
+        density, direct, amplitude, in_sem = refs
+    elif place == "held":
+        density_out, direct, amplitude, density, out_sem = refs
     else:
         density_out, direct, amplitude, density, out_sem, in_sem = refs
+    fetched = prior and place != "held"
     slabs, local, _, slab = own[0][0].shape
     rows = sum(piece.shape[2] for piece in own[0])
     width = sum(piece.shape[2] for piece in groups[0])
-    wide, span = local * rows, local * width
+    wide = local * rows
     total = parts * local
     step = slabs * slab // tiles
-    fresh = [part for part in range(len(groups)) if part or stage != 2]
-    starts = {part: (0 if part == 0 else ((parts if stage != 2 else 0) + part - 1) * wide) for part in fresh}
+    joined = total * width <= 256
 
     def tile_copy(start, inward):
         columns = pl.ds(start * step, step)
@@ -98,7 +96,7 @@
             return pltpu.make_async_copy(density_in.at[:, :, columns], density.at[:, :, columns], in_sem.at[start])
         return pltpu.make_async_copy(density.at[:, :, columns], density_out.at[:, :, columns], out_sem.at[start])
 
-    if density_in is not None:
+    if fetched:
         for start in range(tiles):
             tile_copy(start, True).start()
 
@@ -113,11 +111,15 @@
     def depth_step(k, carry):
         some = slabs // steps
         all_rows = stack([line for block in own for line in lines(block, k * some, some)])
-        for part in fresh:
+        if joined:
+            right = stack([line for group in groups for line in lines(group, k * some, some)])
+            direct[...] = direct[...] + lax.dot_general(all_rows, right, across, preferred_element_type=jnp.float32)
+            return carry
+        for part in range(parts):
             left = all_rows if part == 0 else all_rows[:wide]
             right = stack(lines(groups[part], k * some, some))
             term = lax.dot_general(left, right, across, preferred_element_type=jnp.float32)
-            at = pl.ds(starts[part], left.shape[0])
+            at = pl.ds(0 if part == 0 else (parts + part - 1) * wide, left.shape[0])
             direct[at, :] = direct[at, :] + term
         return carry
 
@@ -125,29 +127,31 @@
     lax.fori_loop(0, steps, depth_step, 0)
     vir_pair = own_vir[...] + vir_rows[number][:, :width]
 
-    def tile(row, column, array=direct):
-        sums = array[row * rows : (row + 1) * rows, column * width : (column + 1) * width]
-        return sums.astype(jnp.bfloat16).astype(jnp.float32)
-
+    def tile(row, column=None):
+        columns = slice(None) if column is None else slice(column * width, (column + 1) * width)
+        return direct[row * rows : (row + 1) * rows, columns].astype(jnp.bfloat16).astype(jnp.float32)
+
+    lanes = lax.broadcasted_iota(jnp.int32, (1, total * width), 1) // width
     for i in range(local):
-        for part in fresh:
-            for k in range(local):
-                j = part * local + k
-                divisor = (occ_pairs[i * total + j][:, :width] - vir_pair).astype(jnp.float32) * energy_unit
-                straight = tile(starts[part] // rows + i, k)
-                crossed = tile(j - local, i, near_swapped) if stage == 2 else tile(j, i)
-                here = slice(j * width, (j + 1) * width)
-                top = 2.0 * straight - crossed
-                amplitude[i * rows : (i + 1) * rows, here] = (top / divisor).astype(jnp.bfloat16)
-    if density_in is not None:
+        if joined:
+            crossed = None
+            for j in range(total):
+                line = tile(j) if i == j else pltpu.roll(tile(j), (j - i) % total * width, 1)
+                crossed = line if crossed is None else jnp.where(lanes == j, line, crossed)
+            pairs = stack([occ_pairs[i * total + j][:, :width] for j in range(total)], 1)
+            divisor = (pairs - stack([vir_pair] * total, 1)).astype(jnp.float32) * energy_unit
+            amplitude[i * rows : (i + 1) * rows, :] = ((2.0 * tile(i) - crossed) / divisor).astype(jnp.bfloat16)
+            continue
+        for j in range(total):
+            part, k = j // local, j % local
+            divisor = (occ_pairs[i * total + j][:, :width] - vir_pair).astype(jnp.float32) * energy_unit
+            top = 2.0 * tile(i if part == 0 else (parts + part - 1) * local + i, k) - tile(j, i)
+            here = slice(j * width, (j + 1) * width)
+            amplitude[i * rows : (i + 1) * rows, here] = (top / divisor).astype(jnp.bfloat16)
+    if fetched:
         for start in range(tiles):
             tile_copy(start, True).wait()
-    if stage == 1:
-        swapped_out[...] = direct[wide:, :].astype(jnp.bfloat16)
-        return
-    if stage == 2:
-        amplitude[:, :span] = near_amplitude[...]
-    prior_ref = held if stage == 2 else density if density_in is not None else None
+    prior_ref = density_in if place == "held" else density if prior else None
     for start in range(tiles):
         columns = slice(start * step, (start + 1) * step)
         some = slabs // tiles
@@ -155,62 +159,50 @@
         term = lax.dot_general(amplitude[...], factor, along, preferred_element_type=jnp.float32)
         term = term.reshape(local, rows, step)
         density[:, :, columns] = term if prior_ref is None else prior_ref[:, :, columns] + term
-        tile_copy(start, False).start()
-    for start in range(tiles):
-        tile_copy(start, False).wait()
-
-
-def block_step(number, energies, own, pieces, density, stage=None, near=()):
+        if place != "keep":
+            tile_copy(start, False).start()
+    if place != "keep":
+        for start in range(tiles):
+            tile_copy(start, False).wait()
+
+
+def block_step(number, energies, own, pieces, density, place=None):
     parts = len(own)
     slabs, local, _, slab = own[0][0].shape
     rows = sum(piece.shape[2] for piece in own[0])
     vmem = pl.BlockSpec(memory_space=pltpu.VMEM)
     hbm = pl.BlockSpec(memory_space=pltpu.HBM)
-    groups = 1 if stage == 1 else parts
-    own = own[:1] if stage == 2 else own
-    operands = [*energies, *[piece for block in own for piece in block], *pieces, *near]
+    operands = [*energies, *[piece for block in own for piece in block], *pieces]
     specs = [vmem] * len(operands)
     wide, aux = local * rows, slabs * slab
-    span = local * sum(piece.shape[2] for piece in pieces) // groups if pieces else wide
-    tiles = max(k for k in range(1, (last_tiles if stage == 2 else body_tiles) + 1) if slabs % k == 0)
-    steps = 1 if stage == 1 else max(k for k in range(1, body_steps + 1) if slabs % k == 0)
-    lines = {None: 2 * parts - 1, 1: parts, 2: parts - 1}[stage]
+    span = local * sum(piece.shape[2] for piece in pieces) // parts if pieces else wide
+    tiles = max(k for k in range(1, (last_tiles if place == "held" else body_tiles) + 1) if slabs % k == 0)
+    steps = max(k for k in range(1, body_steps + 1) if slabs % k == 0)
+    joined = parts * span <= 256
     prior = density is not None
-    layout = (number, parts, len(own[0]), len(pieces) // groups, steps, tiles, prior, stage)
-    scratch = [pltpu.VMEM((lines * wide, span), jnp.float32)]
-    out_shape = jax.ShapeDtypeStruct((local, rows, aux), jnp.float32)
-    out_specs = hbm
+    layout = (number, parts, len(own[0]), len(pieces) // parts, steps, tiles, prior, place)
     aliases = {}
     if prior:
-        if stage is None:
+        if place is None:
             aliases = {len(operands): 0}
         operands.append(density)
-        specs.append(hbm)
-    if stage == 1:
-        out_shape = [
-            jax.ShapeDtypeStruct((wide, span), jnp.bfloat16),
-            jax.ShapeDtypeStruct(((parts - 1) * wide, span), jnp.bfloat16),
-            out_shape,
-        ]
-        out_specs = [vmem] * 3
-    else:
-        scratch += [
-            pltpu.VMEM((wide, parts * span), jnp.bfloat16),
-            pltpu.VMEM((local, rows, aux), jnp.float32),
-            pltpu.SemaphoreType.DMA((tiles,)),
-        ]
-    scratch.append(pltpu.SemaphoreType.DMA((tiles,)))
-    products = lines + (0 if stage == 1 else parts)
+        specs.append(vmem if place == "held" else hbm)
+    sums = (parts * wide, parts * span) if joined else ((2 * parts - 1) * wide, span)
+    scratch = [pltpu.VMEM(sums, jnp.float32), pltpu.VMEM((wide, parts * span), jnp.bfloat16)]
+    if place != "keep":
+        scratch += [pltpu.VMEM((local, rows, aux), jnp.float32), pltpu.SemaphoreType.DMA((tiles,))]
+    if place != "held":
+        scratch.append(pltpu.SemaphoreType.DMA((tiles,)))
     return pl.pallas_call(
         functools.partial(block_kernel, layout),
-        out_shape=out_shape,
+        out_shape=jax.ShapeDtypeStruct((local, rows, aux), jnp.float32),
         in_specs=specs,
-        out_specs=out_specs,
+        out_specs=vmem if place == "keep" else hbm,
         scratch_shapes=scratch,
         input_output_aliases=aliases,
         compiler_params=pltpu.CompilerParams(vmem_limit_bytes=24 * 1024 * 1024),
         cost_estimate=pl.CostEstimate(
-            flops=2 * products * wide * span * aux,
+            flops=2 * (3 * parts - 1) * wide * span * aux,
             bytes_accessed=2 * (parts * (span + wide) + 4 * wide) * aux,
             transcendentals=0,
         ),
@@ -270,11 +262,8 @@
 
     density = block_step(0, energies, own, [], None)
     for number, block in enumerate(blocks, 1):
-        if number < len(blocks):
-            density = block_step(number, energies, own, block, density)
-        else:
-            near = block_step(number, energies, own, block[: len(links)], density, 1)
-            density = block_step(number, energies, own, block, None, 2, near)
+        place = {len(blocks) - 1: "keep", len(blocks): "held"}.get(number)
+        density = block_step(number, energies, own, block, density, place)
     return density
 
 

time: 171 us -> 168 us (0.982)
  Pallas kernels: 45.4 us -> 42.5 us
    pallas_call x10 -> x9, Pallas kernels: 44.6 us -> 41.7 us  [block_step(): pl.pallas_call(functools.partial(block_kernel, layout), out_shape=jax.Sha...]
  transfers between devices with their start and end apart: 34 -> 34, of which waited for: 10 -> 10; matrix products, arithmetic and copies ran while one was open for 10% -> 10% of each run, Pallas kernels for 24% -> 22%
where the time goes in v1:
time: 168 us
  waiting for transfers between devices  78.8 us (47%)
  Pallas kernels  42.5 us (25%)
  starting transfers between devices  22.8 us (14%)
  local copies, waits for them, and re-layouts  21.8 us (13%)
    ppermute x16, waiting for transfers between devices, on_device(): held[way][step] = lax.ppermute(source, 'vir', links[way])  78.7 us
    pallas_call x9, Pallas kernels, block_step(): pl.pallas_call(functools.partial(block_kernel, layout), out_shape=jax.Sha...  41.7 us
    ppermute x16, starting transfers between devices, on_device(): held[way][step] = lax.ppermute(source, 'vir', links[way])  19.8 us
    gather x1, local copies, waits for them, and re-layouts, on_device(): vir_rows = energy_table[away + count, inner][:, None, :]  7.21 us
    unnamed x32, local copies, waits for them, and re-layouts  6.85 us
    slice x2, local copies, waits for them, and re-layouts, on_device(): lax.slice_in_dim(source, some * (step - at), some * (step - at + 1), axis=2)  4.14 us
  transfers between devices with their start and end apart: 34, of which 10 were waited for; matrix products, arithmetic and copies ran while one was open for 10% of the time, Pallas kernels for 22%

profile of v1, /device:TPU:0, one launch (start us, length us, event | category | flops | bytes accessed | tf_op | source)
XLA Modules:
  0.0 167.8 jit_solution(11180942303381731790)
XLA Ops:
  0.0 1.4 copy-done.1
  1.4 0.8 cut.1
  2.2 0.6 collective-permute-start
  2.8 2.6 %collective-permute-start.2 = (bf16[12,2,64,256]{3,2,1,0:T(8,128)(2,1)S(1)}, bf16[12,2,64,256]{3,2,1,0:T(8,128)(2,1)S(1)}, u32[]{:S(2)}, u32[]{:S(2)}) collective-permute-start(bf16[12,2,64,256]{3,2,1,0:T(8,128)(2,1)S(1)} %get-tuple-element.7.refs_0_), channel_id=1, source_target_pairs={{0,2},{2,4},{4,6},{6,7},{7,5},{5,3},{3,1},{1,0},{8,10},{10,12},{12... | collective-permute-start | bytes 2359304 | tf_op jit(solution)/shard_map/ppermute | solution.py:240
  5.4 2.0 %collective-permute-start.16 = (bf16[12,2,64,256]{3,2,1,0:T(8,128)(2,1)S(1)}, bf16[12,2,64,256]{3,2,1,0:T(8,128)(2,1)}, u32[]{:S(2)}, u32[]{:S(2)}) collective-permute-start(bf16[12,2,64,256]{3,2,1,0:T(8,128)(2,1)S(1)} %get-tuple-element.8.refs_1_), channel_id=1, source_target_pairs={{0,2},{2,4},{4,6},{6,7},{7,5},{5,3},{3,1},{1,0},{8,10},{10,12},{12... | collective-permute-start | bytes 2359304 | tf_op jit(solution)/shard_map/ppermute | solution.py:240
  7.5 0.1 collective-permute-start.19
  7.6 16.2 %collective-permute-done.2.refs_4_ = bf16[12,2,64,256]{3,2,1,0:T(8,128)(2,1)S(1)} collective-permute-done((bf16[12,2,64,256]{3,2,1,0:T(8,128)(2,1)S(1)}, bf16[12,2,64,256]{3,2,1,0:T(8,128)(2,1)S(1)}, u32[]{:S(2)}, u32[]{:S(2)}) %collective-permute-start.2) | collective-permute-done | bytes 786464 | tf_op jit(solution)/shard_map/ppermute | solution.py:240
  23.8 2.1 %collective-permute-done.6.refs_5_ = bf16[12,2,64,256]{3,2,1,0:T(8,128)(2,1)S(1)} collective-permute-done((bf16[12,2,64,256]{3,2,1,0:T(8,128)(2,1)S(1)}, bf16[12,2,64,256]{3,2,1,0:T(8,128)(2,1)S(1)}, u32[]{:S(2)}, u32[]{:S(2)}) %collective-permute-start.6) | collective-permute-done | bytes 786464 | tf_op jit(solution)/shard_map/ppermute | solution.py:240
  25.8 14.6 %collective-permute-done.16.refs_4_ = bf16[12,2,64,256]{3,2,1,0:T(8,128)(2,1)} collective-permute-done((bf16[12,2,64,256]{3,2,1,0:T(8,128)(2,1)S(1)}, bf16[12,2,64,256]{3,2,1,0:T(8,128)(2,1)}, u32[]{:S(2)}, u32[]{:S(2)}) %collective-permute-start.16) | collective-permute-done | bytes 786464 | tf_op jit(solution)/shard_map/ppermute | solution.py:240
  40.5 1.8 %collective-permute-start.3 = (bf16[12,2,64,256]{3,2,1,0:T(8,128)(2,1)S(1)}, bf16[12,2,64,256]{3,2,1,0:T(8,128)(2,1)}, u32[]{:S(2)}, u32[]{:S(2)}) collective-permute-start(bf16[12,2,64,256]{3,2,1,0:T(8,128)(2,1)S(1)} %collective-permute-done.2.refs_4_), channel_id=1, source_target_pairs={{0,2},{2,4},{4,6},{6,7},{7,5},{5,3},{3,1},{1,0},{8,10},{10,12},{12... | collective-permute-start | bytes 2359304 | tf_op jit(solution)/shard_map/ppermute | solution.py:240
  42.3 0.9 copy-done.2
  43.2 0.2 collective-permute-start.7
  43.4 0.9 copy-done.4
  44.3 0.9 copy-done.6
  45.2 0.9 copy-done.8
  46.1 1.8 %collective-permute-start.17 = (bf16[12,2,64,256]{3,2,1,0:T(8,128)(2,1)}, bf16[12,2,64,256]{3,2,1,0:T(8,128)(2,1)}, u32[]{:S(2)}, u32[]{:S(2)}) collective-permute-start(bf16[12,2,64,256]{3,2,1,0:T(8,128)(2,1)} %collective-permute-done.16.refs_4_), channel_id=1, source_target_pairs={{0,2},{2,4},{4,6},{6,7},{7,5},{5,3},{3,1},{1,0},{8,10},{10,12},{12... | collective-permute-start | bytes 2359304 | tf_op jit(solution)/shard_map/ppermute | solution.py:240
  47.9 0.9 copy-done.10
  48.8 0.2 collective-permute-start.20
  49.0 12.0 %collective-permute-done.3.refs_4_ = bf16[12,2,64,256]{3,2,1,0:T(8,128)(2,1)} collective-permute-done((bf16[12,2,64,256]{3,2,1,0:T(8,128)(2,1)S(1)}, bf16[12,2,64,256]{3,2,1,0:T(8,128)(2,1)}, u32[]{:S(2)}, u32[]{:S(2)}) %collective-permute-start.3) | collective-permute-done | bytes 786464 | tf_op jit(solution)/shard_map/ppermute | solution.py:240
  61.0 2.7 %collective-permute-done.7.refs_5_ = bf16[12,2,64,256]{3,2,1,0:T(8,128)(2,1)} collective-permute-done((bf16[12,2,64,256]{3,2,1,0:T(8,128)(2,1)S(1)}, bf16[12,2,64,256]{3,2,1,0:T(8,128)(2,1)}, u32[]{:S(2)}, u32[]{:S(2)}) %collective-permute-start.7) | collective-permute-done | bytes 786464 | tf_op jit(solution)/shard_map/ppermute | solution.py:240
  63.7 0.9 copy-done.12
  64.6 1.6 collective-permute-start.4
  66.2 0.8 pad_add_fusion
  67.0 0.1 dynamic_slice.10
  67.1 1.3 dynamic_slice.12
  68.3 0.6 fusion.1
  69.0 8.9 %collective-permute-done.17.refs_4_ = bf16[12,2,64,256]{3,2,1,0:T(8,128)(2,1)} collective-permute-done((bf16[12,2,64,256]{3,2,1,0:T(8,128)(2,1)}, bf16[12,2,64,256]{3,2,1,0:T(8,128)(2,1)}, u32[]{:S(2)}, u32[]{:S(2)}) %collective-permute-start.17) | collective-permute-done | bytes 786464 | tf_op jit(solution)/shard_map/ppermute | solution.py:240
  77.9 1.7 %collective-permute-start.8 = (bf16[12,2,64,256]{3,2,1,0:T(8,128)(2,1)}, bf16[12,2,64,256]{3,2,1,0:T(8,128)(2,1)}, u32[]{:S(2)}, u32[]{:S(2)}) collective-permute-start(bf16[12,2,64,256]{3,2,1,0:T(8,128)(2,1)} %collective-permute-done.7.refs_5_), channel_id=1, source_target_pairs={{2,0},{4,2},{6,4},{7,6},{5,7},{3,5},{1,3},{0,1},{10,8},{12,10},{14... | collective-permute-start | bytes 2359304 | tf_op jit(solution)/shard_map/ppermute | solution.py:240
  79.6 0.1 broadcast_add_fusion
  79.7 0.1 collective-permute-done.20.refs_5_
  79.8 0.5 collective-permute-start.27
  80.3 1.3 gather_fusion
  81.6 1.6 collective-permute-start.18
  83.3 11.4 %collective-permute-done.4.refs_4_ = bf16[12,2,64,256]{3,2,1,0:T(8,128)(2,1)} collective-permute-done((bf16[12,2,64,256]{3,2,1,0:T(8,128)(2,1)}, bf16[12,2,64,256]{3,2,1,0:T(8,128)(2,1)}, u32[]{:S(2)}, u32[]{:S(2)}) %collective-permute-start.4) | collective-permute-done | bytes 786464 | tf_op jit(solution)/shard_map/ppermute | solution.py:240
  94.7 1.7 %collective-permute-start.21 = (bf16[12,2,64,256]{3,2,1,0:T(8,128)(2,1)}, bf16[12,2,64,256]{3,2,1,0:T(8,128)(2,1)}, u32[]{:S(2)}, u32[]{:S(2)}) collective-permute-start(bf16[12,2,64,256]{3,2,1,0:T(8,128)(2,1)} %collective-permute-done.20.refs_5_), channel_id=1, source_target_pairs={{2,0},{4,2},{6,4},{7,6},{5,7},{3,5},{1,3},{0,1},{10,8},{12,10},{14... | collective-permute-start | bytes 2359304 | tf_op jit(solution)/shard_map/ppermute | solution.py:240
  96.5 2.1 %fusion.4 = (bf16[12,2,32,256]{3,2,1,0:T(8,128)(2,1)}, bf16[12,2,32,256]{3,2,1,0:T(8,128)(2,1)}) fusion(bf16[12,2,64,256]{3,2,1,0:T(8,128)(2,1)} %collective-permute-done.4.refs_4_), kind=kLoop, calls=%fused_computation.17 | loop fusion | bytes 1572864 | tf_op jit(solution)/shard_map/slice | solution.py:239
  98.5 0.3 collective-permute-start.12
  98.8 2.1 %fusion.3 = (bf16[12,2,32,256]{3,2,1,0:T(8,128)(2,1)}, bf16[12,2,32,256]{3,2,1,0:T(8,128)(2,1)}) fusion(bf16[12,2,64,256]{3,2,1,0:T(8,128)(2,1)} %collective-permute-done.8.refs_5_), kind=kLoop, calls=%fused_computation.16 | loop fusion | bytes 1572864 | tf_op jit(solution)/shard_map/slice | solution.py:239
  100.9 1.7 %collective-permute-start.13 = (bf16[12,2,32,256]{3,2,1,0:T(8,128)(2,1)}, bf16[12,2,32,256]{3,2,1,0:T(8,128)(2,1)}, u32[]{:S(2)}, u32[]{:S(2)}) collective-permute-start(bf16[12,2,32,256]{3,2,1,0:T(8,128)(2,1)} %get-tuple-element.9), channel_id=1, source_target_pairs={{2,0},{4,2},{6,4},{7,6},{5,7},{3,5},{1,3},{0,1},{10,8},{12,10},{14... | collective-permute-start | bytes 1179656 | tf_op jit(solution)/shard_map/ppermute | solution.py:240
  102.6 0.3 collective-permute-start.5
  102.9 8.6 %collective-permute-done.18.refs_4_ = bf16[12,2,64,256]{3,2,1,0:T(8,128)(2,1)} collective-permute-done((bf16[12,2,64,256]{3,2,1,0:T(8,128)(2,1)}, bf16[12,2,64,256]{3,2,1,0:T(8,128)(2,1)}, u32[]{:S(2)}, u32[]{:S(2)}) %collective-permute-start.18) | collective-permute-done | bytes 786464 | tf_op jit(solution)/shard_map/ppermute | solution.py:240
  111.6 0.1 dynamic-slice_bitcast_fusion
  111.6 0.1 add.109
  111.7 0.1 copy.33.own_vir
  111.8 0.6 gather_fusion.1
  112.4 7.2 %gather_fusion.2 = s32[1152]{0:T(1024)S(1)} fusion(s32[16,128]{1,0:T(8,128)S(1)} %gather_fusion.1, s32[1152]{0:T(1024)S(1)} %copy-done.14), kind=kCustom, calls=%fused_computation.2 | custom fusion | bytes 18432 | tf_op jit(solution)/shard_map/gather | solution.py:257
  119.6 0.6 collective-permute-start.25
  120.2 0.1 collective-permute-start.22
  120.3 0.1 broadcast_in_dim.10.occ_pairs
  120.4 3.4 %shard_map.91.refs_8_ = f32[2,128,3072]{2,1,0:T(8,128)S(1)} custom-call(s32[8,1,128]{2,1,0:T(1,128)S(1)} %broadcast_in_dim.10.occ_pairs, s32[128,1]{1,0:T(8,128)S(1)} %copy.33.own_vir, s32[9,1,128]{2,1,0:T(1,128)S(1)} %broadcast_in_dim.25.vir_rows, bf16[12,2,64,256]{3,2,1,0:T(8,128)(2,1)S(1)} %get-tuple-element.7.refs_0_, ...), custom_call_target="tpu_custom_call" | custom-call | flops 2013265920 | bytes 12582912 | tf_op jit(solution)/shard_map/pallas_call | solution.py:196
  123.9 2.0 %collective-permute-start.9 = (bf16[12,2,32,256]{3,2,1,0:T(8,128)(2,1)S(1)}, bf16[12,2,32,256]{3,2,1,0:T(8,128)(2,1)S(1)}, u32[]{:S(2)}, u32[]{:S(2)}) collective-permute-start(bf16[12,2,32,256]{3,2,1,0:T(8,128)(2,1)S(1)} %copy-done.15), channel_id=1, source_target_pairs={{2,0},{4,2},{6,4},{7,6},{5,7},{3,5},{1,3},{0,1},{10,8},{12,10},{14... | collective-permute-start | bytes 1179656 | tf_op jit(solution)/shard_map/ppermute | solution.py:240
  125.9 2.1 %collective-permute-done.5.refs_4_ = bf16[12,2,32,256]{3,2,1,0:T(8,128)(2,1)} collective-permute-done((bf16[12,2,32,256]{3,2,1,0:T(8,128)(2,1)}, bf16[12,2,32,256]{3,2,1,0:T(8,128)(2,1)}, u32[]{:S(2)}, u32[]{:S(2)}) %collective-permute-start.5) | collective-permute-done | bytes 393248 | tf_op jit(solution)/shard_map/ppermute | solution.py:240
  128.0 3.7 %shard_map.92.refs_8_ = f32[2,128,3072]{2,1,0:T(8,128)S(1)} custom-call(s32[8,1,128]{2,1,0:T(1,128)S(1)} %broadcast_in_dim.10.occ_pairs, s32[128,1]{1,0:T(8,128)S(1)} %copy.33.own_vir, s32[9,1,128]{2,1,0:T(1,128)S(1)} %broadcast_in_dim.25.vir_rows, bf16[12,2,64,256]{3,2,1,0:T(8,128)(2,1)S(1)} %get-tuple-element.7.refs_0_, ...), custom_call_target="tpu_custom_call", output_to_operand_aliasing={{}: (11, {})} | custom-call | flops 2013265920 | bytes 12582912 | tf_op jit(solution)/shard_map/pallas_call | solution.py:196
  131.7 5.1 %shard_map.93.refs_8_ = f32[2,128,3072]{2,1,0:T(8,128)S(1)} custom-call(s32[8,1,128]{2,1,0:T(1,128)S(1)} %broadcast_in_dim.10.occ_pairs, s32[128,1]{1,0:T(8,128)S(1)} %copy.33.own_vir, s32[9,1,128]{2,1,0:T(1,128)S(1)} %broadcast_in_dim.25.vir_rows, bf16[12,2,64,256]{3,2,1,0:T(8,128)(2,1)S(1)} %get-tuple-element.7.refs_0_, ...), custom_call_target="tpu_custom_call", output_to_operand_aliasing={{}: (11, {})} | custom-call | flops 2013265920 | bytes 12582912 | tf_op jit(solution)/shard_map/pallas_call | solution.py:196
  136.8 5.6 %shard_map.94.refs_8_ = f32[2,128,3072]{2,1,0:T(8,128)S(1)} custom-call(s32[8,1,128]{2,1,0:T(1,128)S(1)} %broadcast_in_dim.10.occ_pairs, s32[128,1]{1,0:T(8,128)S(1)} %copy.33.own_vir, s32[9,1,128]{2,1,0:T(1,128)S(1)} %broadcast_in_dim.25.vir_rows, bf16[12,2,64,256]{3,2,1,0:T(8,128)(2,1)S(1)} %get-tuple-element.7.refs_0_, ...), custom_call_target="tpu_custom_call", output_to_operand_aliasing={{}: (11, {})} | custom-call | flops 2013265920 | bytes 12582912 | tf_op jit(solution)/shard_map/pallas_call | solution.py:196
  142.4 0.6 collective-permute-start.14
  143.0 0.1 collective-permute-start.15
  143.0 5.5 %shard_map.95.refs_8_ = f32[2,128,3072]{2,1,0:T(8,128)S(1)} custom-call(s32[8,1,128]{2,1,0:T(1,128)S(1)} %broadcast_in_dim.10.occ_pairs, s32[128,1]{1,0:T(8,128)S(1)} %copy.33.own_vir, s32[9,1,128]{2,1,0:T(1,128)S(1)} %broadcast_in_dim.25.vir_rows, bf16[12,2,64,256]{3,2,1,0:T(8,128)(2,1)S(1)} %get-tuple-element.7.refs_0_, ...), custom_call_target="tpu_custom_call", output_to_operand_aliasing={{}: (11, {})} | custom-call | flops 2013265920 | bytes 12582912 | tf_op jit(solution)/shard_map/pallas_call | solution.py:196
  148.6 0.5 collective-permute-start.10
  149.1 0.1 collective-permute-start.11
  149.2 5.3 %shard_map.96.refs_8_ = f32[2,128,3072]{2,1,0:T(8,128)S(1)} custom-call(s32[8,1,128]{2,1,0:T(1,128)S(1)} %broadcast_in_dim.10.occ_pairs, s32[128,1]{1,0:T(8,128)S(1)} %copy.33.own_vir, s32[9,1,128]{2,1,0:T(1,128)S(1)} %broadcast_in_dim.25.vir_rows, bf16[12,2,64,256]{3,2,1,0:T(8,128)(2,1)S(1)} %get-tuple-element.7.refs_0_, ...), custom_call_target="tpu_custom_call", output_to_operand_aliasing={{}: (11, {})} | custom-call | flops 2013265920 | bytes 12582912 | tf_op jit(solution)/shard_map/pallas_call | solution.py:196
  154.5 5.1 %shard_map.97.refs_8_ = f32[2,128,3072]{2,1,0:T(8,128)S(1)} custom-call(s32[8,1,128]{2,1,0:T(1,128)S(1)} %broadcast_in_dim.10.occ_pairs, s32[128,1]{1,0:T(8,128)S(1)} %copy.33.own_vir, s32[9,1,128]{2,1,0:T(1,128)S(1)} %broadcast_in_dim.25.vir_rows, bf16[12,2,64,256]{3,2,1,0:T(8,128)(2,1)S(1)} %get-tuple-element.7.refs_0_, ...), custom_call_target="tpu_custom_call", output_to_operand_aliasing={{}: (11, {})} | custom-call | flops 2013265920 | bytes 12582912 | tf_op jit(solution)/shard_map/pallas_call | solution.py:196
  159.6 3.6 %shard_map.98.refs_8_ = f32[2,128,3072]{2,1,0:T(8,128)S(1)} custom-call(s32[8,1,128]{2,1,0:T(1,128)S(1)} %broadcast_in_dim.10.occ_pairs, s32[128,1]{1,0:T(8,128)S(1)} %copy.33.own_vir, s32[9,1,128]{2,1,0:T(1,128)S(1)} %broadcast_in_dim.25.vir_rows, bf16[12,2,64,256]{3,2,1,0:T(8,128)(2,1)S(1)} %get-tuple-element.7.refs_0_, ...), custom_call_target="tpu_custom_call" | custom-call | flops 1006632960 | bytes 11010048 | tf_op jit(solution)/shard_map/pallas_call | solution.py:196
  163.2 4.4 %shard_map.99 = f32[2,128,3072]{2,1,0:T(8,128)} custom-call(s32[8,1,128]{2,1,0:T(1,128)S(1)} %broadcast_in_dim.10.occ_pairs, s32[128,1]{1,0:T(8,128)S(1)} %copy.33.own_vir, s32[9,1,128]{2,1,0:T(1,128)S(1)} %broadcast_in_dim.25.vir_rows, bf16[12,2,64,256]{3,2,1,0:T(8,128)(2,1)S(1)} %get-tuple-element.7.refs_0_, ...), custom_call_target="tpu_custom_call" | custom-call | flops 1006632960 | bytes 11010048 | tf_op jit(solution)/shard_map/pallas_call | solution.py:196
  (64 shorter events, 0.2 us)
Async XLA Ops:
  0.0 111.6 %copy-start = (s32[1024]{0:T(1024)S(1)}, s32[1024]{0:T(1024)}, u32[]{:S(2)}) copy-start(s32[1024]{0:T(1024)} %param.11) | copy-start | bytes 12292
  0.0 1.4 copy-start.1
  1.4 111.0 %copy-start.14 = (s32[1152]{0:T(1024)S(1)}, s32[1152]{0:T(1024)}, u32[]{:S(2)}) copy-start(s32[1152]{0:T(1024)} %constant.98) | copy-start | bytes 13828
  2.2 5.2 %collective-permute-start = (bf16[12,2,64,256]{3,2,1,0:T(8,128)(2,1)S(1)}, bf16[12,2,64,256]{3,2,1,0:T(8,128)(2,1)S(1)}, u32[]{:S(2)}, u32[]{:S(2)}) collective-permute-start(bf16[12,2,64,256]{3,2,1,0:T(8,128)(2,1)S(1)} %get-tuple-element.7.refs_0_), channel_id=1, source_target_pairs={{8,0},{0,8},{9,1},{1,9},{10,2},{2,10},{11,3},{3,11},{12,4},{4,12},... | collective-permute-start | bytes 2359304 | tf_op jit(solution)/shard_map/ppermute | solution.py:227
  2.8 21.0 %collective-permute-start.2 = (bf16[12,2,64,256]{3,2,1,0:T(8,128)(2,1)S(1)}, bf16[12,2,64,256]{3,2,1,0:T(8,128)(2,1)S(1)}, u32[]{:S(2)}, u32[]{:S(2)}) collective-permute-start(bf16[12,2,64,256]{3,2,1,0:T(8,128)(2,1)S(1)} %get-tuple-element.7.refs_0_), channel_id=1, source_target_pairs={{0,2},{2,4},{4,6},{6,7},{7,5},{5,3},{3,1},{1,0},{8,10},{10,12},{12... | collective-permute-start | bytes 2359304 | tf_op jit(solution)/shard_map/ppermute | solution.py:240
  5.4 20.4 %collective-permute-start.6 = (bf16[12,2,64,256]{3,2,1,0:T(8,128)(2,1)S(1)}, bf16[12,2,64,256]{3,2,1,0:T(8,128)(2,1)S(1)}, u32[]{:S(2)}, u32[]{:S(2)}) collective-permute-start(bf16[12,2,64,256]{3,2,1,0:T(8,128)(2,1)S(1)} %get-tuple-element.8.refs_1_), channel_id=1, source_target_pairs={{2,0},{4,2},{6,4},{7,6},{5,7},{3,5},{1,3},{0,1},{10,8},{12,10},{14... | collective-permute-start | bytes 2359304 | tf_op jit(solution)/shard_map/ppermute | solution.py:240
  5.4 35.0 %collective-permute-start.16 = (bf16[12,2,64,256]{3,2,1,0:T(8,128)(2,1)S(1)}, bf16[12,2,64,256]{3,2,1,0:T(8,128)(2,1)}, u32[]{:S(2)}, u32[]{:S(2)}) collective-permute-start(bf16[12,2,64,256]{3,2,1,0:T(8,128)(2,1)S(1)} %get-tuple-element.8.refs_1_), channel_id=1, source_target_pairs={{0,2},{2,4},{4,6},{6,7},{7,5},{5,3},{3,1},{1,0},{8,10},{10,12},{12... | collective-permute-start | bytes 2359304 | tf_op jit(solution)/shard_map/ppermute | solution.py:240
  7.4 33.0 %collective-permute-start.1 = (bf16[12,2,64,256]{3,2,1,0:T(8,128)(2,1)S(1)}, bf16[12,2,64,256]{3,2,1,0:T(8,128)(2,1)S(1)}, u32[]{:S(2)}, u32[]{:S(2)}) collective-permute-start(bf16[12,2,64,256]{3,2,1,0:T(8,128)(2,1)S(1)} %get-tuple-element.8.refs_1_), channel_id=1, source_target_pairs={{8,0},{0,8},{9,1},{1,9},{10,2},{2,10},{11,3},{3,11},{12,4},{4,12},... | collective-permute-start | bytes 2359304 | tf_op jit(solution)/shard_map/ppermute | solution.py:227
  7.5 35.7 %collective-permute-start.19 = (bf16[12,2,64,256]{3,2,1,0:T(8,128)(2,1)S(1)}, bf16[12,2,64,256]{3,2,1,0:T(8,128)(2,1)}, u32[]{:S(2)}, u32[]{:S(2)}) collective-permute-start(bf16[12,2,64,256]{3,2,1,0:T(8,128)(2,1)S(1)} %get-tuple-element.7.refs_0_), channel_id=1, source_target_pairs={{2,0},{4,2},{6,4},{7,6},{5,7},{3,5},{1,3},{0,1},{10,8},{12,10},{14... | collective-permute-start | bytes 2359304 | tf_op jit(solution)/shard_map/ppermute | solution.py:240
  23.8 20.6 %collective-permute-start.32 = (bf16[12,2,64,256]{3,2,1,0:T(8,128)(2,1)S(1)}, bf16[12,2,64,256]{3,2,1,0:T(8,128)(2,1)S(1)}, u32[]{:S(2)}, u32[]{:S(2)}) collective-permute-start(bf16[12,2,64,256]{3,2,1,0:T(8,128)(2,1)S(1)} %collective-permute-done.2.refs_4_), channel_id=1, source_target_pairs={{8,0},{0,8},{9,1},{1,9},{10,2},{2,10},{11,3},{3,11},{12,4},{4,12},... | collective-permute-start | bytes 2359304 | tf_op jit(solution)/shard_map/ppermute | solution.py:245
  25.8 19.4 %collective-permute-start.33 = (bf16[12,2,64,256]{3,2,1,0:T(8,128)(2,1)S(1)}, bf16[12,2,64,256]{3,2,1,0:T(8,128)(2,1)S(1)}, u32[]{:S(2)}, u32[]{:S(2)}) collective-permute-start(bf16[12,2,64,256]{3,2,1,0:T(8,128)(2,1)S(1)} %collective-permute-done.6.refs_5_), channel_id=1, source_target_pairs={{8,0},{0,8},{9,1},{1,9},{10,2},{2,10},{11,3},{3,11},{12,4},{4,12},... | collective-permute-start | bytes 2359304 | tf_op jit(solution)/shard_map/ppermute | solution.py:245
  40.5 7.5 %collective-permute-start.30 = (bf16[12,2,64,256]{3,2,1,0:T(8,128)(2,1)}, bf16[12,2,64,256]{3,2,1,0:T(8,128)(2,1)S(1)}, u32[]{:S(2)}, u32[]{:S(2)}) collective-permute-start(bf16[12,2,64,256]{3,2,1,0:T(8,128)(2,1)} %collective-permute-done.16.refs_4_), channel_id=1, source_target_pairs={{8,0},{0,8},{9,1},{1,9},{10,2},{2,10},{11,3},{3,11},{12,4},{4,12},... | collective-permute-start | bytes 2359304 | tf_op jit(solution)/shard_map/ppermute | solution.py:245
  40.5 20.5 %collective-permute-start.3 = (bf16[12,2,64,256]{3,2,1,0:T(8,128)(2,1)S(1)}, bf16[12,2,64,256]{3,2,1,0:T(8,128)(2,1)}, u32[]{:S(2)}, u32[]{:S(2)}) collective-permute-start(bf16[12,2,64,256]{3,2,1,0:T(8,128)(2,1)S(1)} %collective-permute-done.2.refs_4_), channel_id=1, source_target_pairs={{0,2},{2,4},{4,6},{6,7},{7,5},{5,3},{3,1},{1,0},{8,10},{10,12},{12... | collective-permute-start | bytes 2359304 | tf_op jit(solution)/shard_map/ppermute | solution.py:240
  42.3 0.9 copy-start.2
  43.2 20.5 %collective-permute-start.7 = (bf16[12,2,64,256]{3,2,1,0:T(8,128)(2,1)S(1)}, bf16[12,2,64,256]{3,2,1,0:T(8,128)(2,1)}, u32[]{:S(2)}, u32[]{:S(2)}) collective-permute-start(bf16[12,2,64,256]{3,2,1,0:T(8,128)(2,1)S(1)} %collective-permute-done.6.refs_5_), channel_id=1, source_target_pairs={{2,0},{4,2},{6,4},{7,6},{5,7},{3,5},{1,3},{0,1},{10,8},{12,10},{14... | collective-permute-start | bytes 2359304 | tf_op jit(solution)/shard_map/ppermute | solution.py:240
  43.4 0.9 copy-start.4
  44.3 0.9 copy-start.6
  45.2 18.5 %collective-permute-start.31 = (bf16[12,2,64,256]{3,2,1,0:T(8,128)(2,1)}, bf16[12,2,64,256]{3,2,1,0:T(8,128)(2,1)S(1)}, u32[]{:S(2)}, u32[]{:S(2)}) collective-permute-start(bf16[12,2,64,256]{3,2,1,0:T(8,128)(2,1)} %collective-permute-done.19.refs_5_), channel_id=1, source_target_pairs={{8,0},{0,8},{9,1},{1,9},{10,2},{2,10},{11,3},{3,11},{12,4},{4,12},... | collective-permute-start | bytes 2359304 | tf_op jit(solution)/shard_map/ppermute | solution.py:245
  45.2 0.9 copy-start.8
  46.1 31.7 %collective-permute-start.17 = (bf16[12,2,64,256]{3,2,1,0:T(8,128)(2,1)}, bf16[12,2,64,256]{3,2,1,0:T(8,128)(2,1)}, u32[]{:S(2)}, u32[]{:S(2)}) collective-permute-start(bf16[12,2,64,256]{3,2,1,0:T(8,128)(2,1)} %collective-permute-done.16.refs_4_), channel_id=1, source_target_pairs={{0,2},{2,4},{4,6},{6,7},{7,5},{5,3},{3,1},{1,0},{8,10},{10,12},{12... | collective-permute-start | bytes 2359304 | tf_op jit(solution)/shard_map/ppermute | solution.py:240
  47.9 0.9 copy-start.10
  48.8 31.0 %collective-permute-start.20 = (bf16[12,2,64,256]{3,2,1,0:T(8,128)(2,1)}, bf16[12,2,64,256]{3,2,1,0:T(8,128)(2,1)}, u32[]{:S(2)}, u32[]{:S(2)}) collective-permute-start(bf16[12,2,64,256]{3,2,1,0:T(8,128)(2,1)} %collective-permute-done.19.refs_5_), channel_id=1, source_target_pairs={{2,0},{4,2},{6,4},{7,6},{5,7},{3,5},{1,3},{0,1},{10,8},{12,10},{14... | collective-permute-start | bytes 2359304 | tf_op jit(solution)/shard_map/ppermute | solution.py:240
  61.0 18.8 %collective-permute-start.28 = (bf16[12,2,64,256]{3,2,1,0:T(8,128)(2,1)}, bf16[12,2,64,256]{3,2,1,0:T(8,128)(2,1)}, u32[]{:S(2)}, u32[]{:S(2)}) collective-permute-start(bf16[12,2,64,256]{3,2,1,0:T(8,128)(2,1)} %collective-permute-done.3.refs_4_), channel_id=1, source_target_pairs={{8,0},{0,8},{9,1},{1,9},{10,2},{2,10},{11,3},{3,11},{12,4},{4,12},... | collective-permute-start | bytes 2359304 | tf_op jit(solution)/shard_map/ppermute | solution.py:245
  63.7 17.9 %collective-permute-start.29 = (bf16[12,2,64,256]{3,2,1,0:T(8,128)(2,1)}, bf16[12,2,64,256]{3,2,1,0:T(8,128)(2,1)}, u32[]{:S(2)}, u32[]{:S(2)}) collective-permute-start(bf16[12,2,64,256]{3,2,1,0:T(8,128)(2,1)} %collective-permute-done.7.refs_5_), channel_id=1, source_target_pairs={{8,0},{0,8},{9,1},{1,9},{10,2},{2,10},{11,3},{3,11},{12,4},{4,12},... | collective-permute-start | bytes 2359304 | tf_op jit(solution)/shard_map/ppermute | solution.py:245
  63.7 0.9 copy-start.12
  64.6 30.1 %collective-permute-start.4 = (bf16[12,2,64,256]{3,2,1,0:T(8,128)(2,1)}, bf16[12,2,64,256]{3,2,1,0:T(8,128)(2,1)}, u32[]{:S(2)}, u32[]{:S(2)}) collective-permute-start(bf16[12,2,64,256]{3,2,1,0:T(8,128)(2,1)} %collective-permute-done.3.refs_4_), channel_id=1, source_target_pairs={{0,2},{2,4},{4,6},{6,7},{7,5},{5,3},{3,1},{1,0},{8,10},{10,12},{12... | collective-permute-start | bytes 2359304 | tf_op jit(solution)/shard_map/ppermute | solution.py:240
  77.9 20.7 %collective-permute-start.8 = (bf16[12,2,64,256]{3,2,1,0:T(8,128)(2,1)}, bf16[12,2,64,256]{3,2,1,0:T(8,128)(2,1)}, u32[]{:S(2)}, u32[]{:S(2)}) collective-permute-start(bf16[12,2,64,256]{3,2,1,0:T(8,128)(2,1)} %collective-permute-done.7.refs_5_), channel_id=1, source_target_pairs={{2,0},{4,2},{6,4},{7,6},{5,7},{3,5},{1,3},{0,1},{10,8},{12,10},{14... | collective-permute-start | bytes 2359304 | tf_op jit(solution)/shard_map/ppermute | solution.py:240
  79.8 21.1 %collective-permute-start.26 = (bf16[12,2,64,256]{3,2,1,0:T(8,128)(2,1)}, bf16[12,2,64,256]{3,2,1,0:T(8,128)(2,1)}, u32[]{:S(2)}, u32[]{:S(2)}) collective-permute-start(bf16[12,2,64,256]{3,2,1,0:T(8,128)(2,1)} %collective-permute-done.17.refs_4_), channel_id=1, source_target_pairs={{8,0},{0,8},{9,1},{1,9},{10,2},{2,10},{11,3},{3,11},{12,4},{4,12},... | collective-permute-start | bytes 2359304 | tf_op jit(solution)/shard_map/ppermute | solution.py:245
  79.8 22.8 %collective-permute-start.27 = (bf16[12,2,64,256]{3,2,1,0:T(8,128)(2,1)}, bf16[12,2,64,256]{3,2,1,0:T(8,128)(2,1)}, u32[]{:S(2)}, u32[]{:S(2)}) collective-permute-start(bf16[12,2,64,256]{3,2,1,0:T(8,128)(2,1)} %collective-permute-done.20.refs_5_), channel_id=1, source_target_pairs={{8,0},{0,8},{9,1},{1,9},{10,2},{2,10},{11,3},{3,11},{12,4},{4,12},... | collective-permute-start | bytes 2359304 | tf_op jit(solution)/shard_map/ppermute | solution.py:245
  81.6 29.9 %collective-permute-start.18 = (bf16[12,2,64,256]{3,2,1,0:T(8,128)(2,1)}, bf16[12,2,64,256]{3,2,1,0:T(8,128)(2,1)}, u32[]{:S(2)}, u32[]{:S(2)}) collective-permute-start(bf16[12,2,64,256]{3,2,1,0:T(8,128)(2,1)} %collective-permute-done.17.refs_4_), channel_id=1, source_target_pairs={{0,2},{2,4},{4,6},{6,7},{7,5},{5,3},{3,1},{1,0},{8,10},{10,12},{12... | collective-permute-start | bytes 2359304 | tf_op jit(solution)/shard_map/ppermute | solution.py:240
  94.7 24.9 %collective-permute-start.21 = (bf16[12,2,64,256]{3,2,1,0:T(8,128)(2,1)}, bf16[12,2,64,256]{3,2,1,0:T(8,128)(2,1)}, u32[]{:S(2)}, u32[]{:S(2)}) collective-permute-start(bf16[12,2,64,256]{3,2,1,0:T(8,128)(2,1)} %collective-permute-done.20.refs_5_), channel_id=1, source_target_pairs={{2,0},{4,2},{6,4},{7,6},{5,7},{3,5},{1,3},{0,1},{10,8},{12,10},{14... | collective-permute-start | bytes 2359304 | tf_op jit(solution)/shard_map/ppermute | solution.py:240
  98.5 21.7 %collective-permute-start.12 = (bf16[12,2,32,256]{3,2,1,0:T(8,128)(2,1)}, bf16[12,2,32,256]{3,2,1,0:T(8,128)(2,1)}, u32[]{:S(2)}, u32[]{:S(2)}) collective-permute-start(bf16[12,2,32,256]{3,2,1,0:T(8,128)(2,1)} %get-tuple-element.11), channel_id=1, source_target_pairs={{0,2},{2,4},{4,6},{6,7},{7,5},{5,3},{3,1},{1,0},{8,10},{10,12},{12... | collective-permute-start | bytes 1179656 | tf_op jit(solution)/shard_map/ppermute | solution.py:240
  100.9 23.0 %collective-permute-start.13 = (bf16[12,2,32,256]{3,2,1,0:T(8,128)(2,1)}, bf16[12,2,32,256]{3,2,1,0:T(8,128)(2,1)}, u32[]{:S(2)}, u32[]{:S(2)}) collective-permute-start(bf16[12,2,32,256]{3,2,1,0:T(8,128)(2,1)} %get-tuple-element.9), channel_id=1, source_target_pairs={{2,0},{4,2},{6,4},{7,6},{5,7},{3,5},{1,3},{0,1},{10,8},{12,10},{14... | collective-permute-start | bytes 1179656 | tf_op jit(solution)/shard_map/ppermute | solution.py:240
  102.6 25.3 %collective-permute-start.5 = (bf16[12,2,32,256]{3,2,1,0:T(8,128)(2,1)}, bf16[12,2,32,256]{3,2,1,0:T(8,128)(2,1)}, u32[]{:S(2)}, u32[]{:S(2)}) collective-permute-start(bf16[12,2,32,256]{3,2,1,0:T(8,128)(2,1)} %get-tuple-element.12), channel_id=1, source_target_pairs={{0,2},{2,4},{4,6},{6,7},{7,5},{5,3},{3,1},{1,0},{8,10},{10,12},{12... | collective-permute-start | bytes 1179656 | tf_op jit(solution)/shard_map/ppermute | solution.py:240
  111.6 31.4 %collective-permute-start.24 = (bf16[12,2,64,256]{3,2,1,0:T(8,128)(2,1)}, bf16[12,2,64,256]{3,2,1,0:T(8,128)(2,1)}, u32[]{:S(2)}, u32[]{:S(2)}) collective-permute-start(bf16[12,2,64,256]{3,2,1,0:T(8,128)(2,1)} %collective-permute-done.4.refs_4_), channel_id=1, source_target_pairs={{8,0},{0,8},{9,1},{1,9},{10,2},{2,10},{11,3},{3,11},{12,4},{4,12},... | collective-permute-start | bytes 2359304 | tf_op jit(solution)/shard_map/ppermute | solution.py:245
  119.6 29.0 %collective-permute-start.25 = (bf16[12,2,64,256]{3,2,1,0:T(8,128)(2,1)}, bf16[12,2,64,256]{3,2,1,0:T(8,128)(2,1)S(1)}, u32[]{:S(2)}, u32[]{:S(2)}) collective-permute-start(bf16[12,2,64,256]{3,2,1,0:T(8,128)(2,1)} %collective-permute-done.8.refs_5_), channel_id=1, source_target_pairs={{8,0},{0,8},{9,1},{1,9},{10,2},{2,10},{11,3},{3,11},{12,4},{4,12},... | collective-permute-start | bytes 2359304 | tf_op jit(solution)/shard_map/ppermute | solution.py:245
  120.2 28.9 %collective-permute-start.22 = (bf16[12,2,64,256]{3,2,1,0:T(8,128)(2,1)}, bf16[12,2,64,256]{3,2,1,0:T(8,128)(2,1)S(1)}, u32[]{:S(2)}, u32[]{:S(2)}) collective-permute-start(bf16[12,2,64,256]{3,2,1,0:T(8,128)(2,1)} %collective-permute-done.18.refs_4_), channel_id=1, source_target_pairs={{8,0},{0,8},{9,1},{1,9},{10,2},{2,10},{11,3},{3,11},{12,4},{4,12},... | collective-permute-start | bytes 2359304 | tf_op jit(solution)/shard_map/ppermute | solution.py:245
  120.4 3.5 %copy-start.15 = (bf16[12,2,32,256]{3,2,1,0:T(8,128)(2,1)S(1)}, bf16[12,2,32,256]{3,2,1,0:T(8,128)(2,1)}, u32[]{:S(2)}) copy-start(bf16[12,2,32,256]{3,2,1,0:T(8,128)(2,1)} %get-tuple-element.10) | copy-start | bytes 1179652
  120.4 7.6 %copy-start.3 = (bf16[12,2,64,256]{3,2,1,0:T(8,128)(2,1)S(1)}, bf16[12,2,64,256]{3,2,1,0:T(8,128)(2,1)}, u32[]{:S(2)}) copy-start(bf16[12,2,64,256]{3,2,1,0:T(8,128)(2,1)} %copy-done.2) | copy-start | bytes 2359300
  120.4 7.6 %copy-start.5 = (bf16[12,2,64,256]{3,2,1,0:T(8,128)(2,1)S(1)}, bf16[12,2,64,256]{3,2,1,0:T(8,128)(2,1)}, u32[]{:S(2)}) copy-start(bf16[12,2,64,256]{3,2,1,0:T(8,128)(2,1)} %copy-done.4) | copy-start | bytes 2359300
  120.4 7.6 %copy-start.7 = (bf16[12,2,64,256]{3,2,1,0:T(8,128)(2,1)S(1)}, bf16[12,2,64,256]{3,2,1,0:T(8,128)(2,1)}, u32[]{:S(2)}) copy-start(bf16[12,2,64,256]{3,2,1,0:T(8,128)(2,1)} %copy-done.6) | copy-start | bytes 2359300
  120.4 7.6 %copy-start.9 = (bf16[12,2,64,256]{3,2,1,0:T(8,128)(2,1)S(1)}, bf16[12,2,64,256]{3,2,1,0:T(8,128)(2,1)}, u32[]{:S(2)}) copy-start(bf16[12,2,64,256]{3,2,1,0:T(8,128)(2,1)} %copy-done.8) | copy-start | bytes 2359300
  123.9 7.8 %copy-start.11 = (bf16[12,2,64,256]{3,2,1,0:T(8,128)(2,1)S(1)}, bf16[12,2,64,256]{3,2,1,0:T(8,128)(2,1)}, u32[]{:S(2)}) copy-start(bf16[12,2,64,256]{3,2,1,0:T(8,128)(2,1)} %copy-done.10) | copy-start | bytes 2359300
  123.9 7.8 %copy-start.13 = (bf16[12,2,64,256]{3,2,1,0:T(8,128)(2,1)S(1)}, bf16[12,2,64,256]{3,2,1,0:T(8,128)(2,1)}, u32[]{:S(2)}) copy-start(bf16[12,2,64,256]{3,2,1,0:T(8,128)(2,1)} %copy-done.12) | copy-start | bytes 2359300
  123.9 18.5 %collective-permute-start.9 = (bf16[12,2,32,256]{3,2,1,0:T(8,128)(2,1)S(1)}, bf16[12,2,32,256]{3,2,1,0:T(8,128)(2,1)S(1)}, u32[]{:S(2)}, u32[]{:S(2)}) collective-permute-start(bf16[12,2,32,256]{3,2,1,0:T(8,128)(2,1)S(1)} %copy-done.15), channel_id=1, source_target_pairs={{2,0},{4,2},{6,4},{7,6},{5,7},{3,5},{1,3},{0,1},{10,8},{12,10},{14... | collective-permute-start | bytes 1179656 | tf_op jit(solution)/shard_map/ppermute | solution.py:240
  128.0 26.6 %collective-permute-start.23 = (bf16[12,2,64,256]{3,2,1,0:T(8,128)(2,1)}, bf16[12,2,64,256]{3,2,1,0:T(8,128)(2,1)S(1)}, u32[]{:S(2)}, u32[]{:S(2)}) collective-permute-start(bf16[12,2,64,256]{3,2,1,0:T(8,128)(2,1)} %collective-permute-done.21.refs_5_), channel_id=1, source_target_pairs={{8,0},{0,8},{9,1},{1,9},{10,2},{2,10},{11,3},{3,11},{12,4},{4,12},... | collective-permute-start | bytes 2359304 | tf_op jit(solution)/shard_map/ppermute | solution.py:245
  142.4 17.2 %collective-permute-start.14 = (bf16[12,2,32,256]{3,2,1,0:T(8,128)(2,1)}, bf16[12,2,32,256]{3,2,1,0:T(8,128)(2,1)S(1)}, u32[]{:S(2)}, u32[]{:S(2)}) collective-permute-start(bf16[12,2,32,256]{3,2,1,0:T(8,128)(2,1)} %collective-permute-done.12.refs_4_), channel_id=1, source_target_pairs={{8,0},{0,8},{9,1},{1,9},{10,2},{2,10},{11,3},{3,11},{12,4},{4,12},... | collective-permute-start | bytes 1179656 | tf_op jit(solution)/shard_map/ppermute | solution.py:245
  143.0 16.7 %collective-permute-start.15 = (bf16[12,2,32,256]{3,2,1,0:T(8,128)(2,1)}, bf16[12,2,32,256]{3,2,1,0:T(8,128)(2,1)S(1)}, u32[]{:S(2)}, u32[]{:S(2)}) collective-permute-start(bf16[12,2,32,256]{3,2,1,0:T(8,128)(2,1)} %collective-permute-done.13.refs_5_), channel_id=1, source_target_pairs={{8,0},{0,8},{9,1},{1,9},{10,2},{2,10},{11,3},{3,11},{12,4},{4,12},... | collective-permute-start | bytes 1179656 | tf_op jit(solution)/shard_map/ppermute | solution.py:245
  148.6 14.6 %collective-permute-start.10 = (bf16[12,2,32,256]{3,2,1,0:T(8,128)(2,1)}, bf16[12,2,32,256]{3,2,1,0:T(8,128)(2,1)S(1)}, u32[]{:S(2)}, u32[]{:S(2)}) collective-permute-start(bf16[12,2,32,256]{3,2,1,0:T(8,128)(2,1)} %collective-permute-done.5.refs_4_), channel_id=1, source_target_pairs={{8,0},{0,8},{9,1},{1,9},{10,2},{2,10},{11,3},{3,11},{12,4},{4,12},... | collective-permute-start | bytes 1179656 | tf_op jit(solution)/shard_map/ppermute | solution.py:245
  149.1 14.1 %collective-permute-start.11 = (bf16[12,2,32,256]{3,2,1,0:T(8,128)(2,1)S(1)}, bf16[12,2,32,256]{3,2,1,0:T(8,128)(2,1)S(1)}, u32[]{:S(2)}, u32[]{:S(2)}) collective-permute-start(bf16[12,2,32,256]{3,2,1,0:T(8,128)(2,1)S(1)} %collective-permute-done.9.refs_5_), channel_id=1, source_target_pairs={{8,0},{0,8},{9,1},{1,9},{10,2},{2,10},{11,3},{3,11},{12,4},{4,12},... | collective-permute-start | bytes 1179656 | tf_op jit(solution)/shard_map/ppermute | solution.py:245

commit v2 on v0

--- a/solution.py
+++ b/solution.py
@@ -14,7 +14,7 @@
 last_cuts = 2
 body_steps = 2
 body_tiles = 3
-last_tiles = 6
+last_tiles = 4
 
 across = (((1,), (1,)), ((), ()))
 along = (((1,), (0,)), ((), ()))
@@ -125,20 +125,23 @@
     lax.fori_loop(0, steps, depth_step, 0)
     vir_pair = own_vir[...] + vir_rows[number][:, :width]
 
-    def tile(row, column, array=direct):
-        sums = array[row * rows : (row + 1) * rows, column * width : (column + 1) * width]
-        return sums.astype(jnp.bfloat16).astype(jnp.float32)
-
+    lanes = lax.broadcasted_iota(jnp.int32, (1, local * width), 1) // width
     for i in range(local):
         for part in fresh:
+            straight = direct[starts[part] + i * rows : starts[part] + (i + 1) * rows, :]
+            straight = straight.astype(jnp.bfloat16).astype(jnp.float32)
+            crossed = None
             for k in range(local):
                 j = part * local + k
-                divisor = (occ_pairs[i * total + j][:, :width] - vir_pair).astype(jnp.float32) * energy_unit
-                straight = tile(starts[part] // rows + i, k)
-                crossed = tile(j - local, i, near_swapped) if stage == 2 else tile(j, i)
-                here = slice(j * width, (j + 1) * width)
-                top = 2.0 * straight - crossed
-                amplitude[i * rows : (i + 1) * rows, here] = (top / divisor).astype(jnp.bfloat16)
+                array, row = (near_swapped, j - local) if stage == 2 else (direct, j)
+                line = array[row * rows : (row + 1) * rows, :].astype(jnp.bfloat16).astype(jnp.float32)
+                if k != i:
+                    line = pltpu.roll(line, (k - i) % local * width, 1)
+                crossed = line if crossed is None else jnp.where(lanes == k, line, crossed)
+            pair = [occ_pairs[i * total + part * local + k][:, :width] for k in range(local)]
+            divisor = (stack(pair, 1) - stack([vir_pair] * local, 1)).astype(jnp.float32) * energy_unit
+            here = slice(part * local * width, (part + 1) * local * width)
+            amplitude[i * rows : (i + 1) * rows, here] = ((2.0 * straight - crossed) / divisor).astype(jnp.bfloat16)
     if density_in is not None:
         for start in range(tiles):
             tile_copy(start, True).wait()

time: 171 us -> 171 us (level)
  no operation moved by 1% of the time
where the time goes in v2:
time: 171 us
  waiting for transfers between devices  78.8 us (46%)
  Pallas kernels  45.4 us (27%)
  starting transfers between devices  22.8 us (13%)
  local copies, waits for them, and re-layouts  21.8 us (13%)
    ppermute x16, waiting for transfers between devices, on_device(): held[way][step] = lax.ppermute(source, 'vir', links[way])  78.8 us
    pallas_call x10, Pallas kernels, block_step(): pl.pallas_call(functools.partial(block_kernel, layout), out_shape=out_sha...  44.6 us
    ppermute x16, starting transfers between devices, on_device(): held[way][step] = lax.ppermute(source, 'vir', links[way])  19.8 us
    gather x1, local copies, waits for them, and re-layouts, on_device(): vir_rows = energy_table[away + count, inner][:, None, :]  7.21 us
    unnamed x32, local copies, waits for them, and re-layouts  6.87 us
    slice x2, local copies, waits for them, and re-layouts, on_device(): lax.slice_in_dim(source, some * (step - at), some * (step - at + 1), axis=2)  4.15 us
  transfers between devices with their start and end apart: 34, of which 10 were waited for; matrix products, arithmetic and copies ran while one was open for 10% of the time, Pallas kernels for 24%

profile of v2, /device:TPU:0, one launch (start us, length us, event | category | flops | bytes accessed | tf_op | source)
XLA Modules:
  0.0 170.7 jit_solution(6349517150502410937)
XLA Ops:
  0.0 1.4 copy-done.1
  1.4 0.8 cut.1
  2.2 0.6 collective-permute-start.10
  2.8 2.6 %collective-permute-start = (bf16[12,2,64,256]{3,2,1,0:T(8,128)(2,1)S(1)}, bf16[12,2,64,256]{3,2,1,0:T(8,128)(2,1)S(1)}, u32[]{:S(2)}, u32[]{:S(2)}) collective-permute-start(bf16[12,2,64,256]{3,2,1,0:T(8,128)(2,1)S(1)} %get-tuple-element.10.refs_0_), channel_id=1, source_target_pairs={{0,2},{2,4},{4,6},{6,7},{7,5},{5,3},{3,1},{1,0},{8,10},{10,12},{12... | collective-permute-start | bytes 2359304 | tf_op jit(solution)/shard_map/ppermute | solution.py:251
  5.4 2.0 %collective-permute-start.16 = (bf16[12,2,64,256]{3,2,1,0:T(8,128)(2,1)S(1)}, bf16[12,2,64,256]{3,2,1,0:T(8,128)(2,1)}, u32[]{:S(2)}, u32[]{:S(2)}) collective-permute-start(bf16[12,2,64,256]{3,2,1,0:T(8,128)(2,1)S(1)} %get-tuple-element.11.refs_1_), channel_id=1, source_target_pairs={{0,2},{2,4},{4,6},{6,7},{7,5},{5,3},{3,1},{1,0},{8,10},{10,12},{12... | collective-permute-start | bytes 2359304 | tf_op jit(solution)/shard_map/ppermute | solution.py:251
  7.5 0.1 collective-permute-start.19
  7.6 16.2 %collective-permute-done.refs_4_ = bf16[12,2,64,256]{3,2,1,0:T(8,128)(2,1)S(1)} collective-permute-done((bf16[12,2,64,256]{3,2,1,0:T(8,128)(2,1)S(1)}, bf16[12,2,64,256]{3,2,1,0:T(8,128)(2,1)S(1)}, u32[]{:S(2)}, u32[]{:S(2)}) %collective-permute-start) | collective-permute-done | bytes 786464 | tf_op jit(solution)/shard_map/ppermute | solution.py:251
  23.8 2.1 %collective-permute-done.4.refs_5_ = bf16[12,2,64,256]{3,2,1,0:T(8,128)(2,1)S(1)} collective-permute-done((bf16[12,2,64,256]{3,2,1,0:T(8,128)(2,1)S(1)}, bf16[12,2,64,256]{3,2,1,0:T(8,128)(2,1)S(1)}, u32[]{:S(2)}, u32[]{:S(2)}) %collective-permute-start.4) | collective-permute-done | bytes 786464 | tf_op jit(solution)/shard_map/ppermute | solution.py:251
  25.8 14.6 %collective-permute-done.16.refs_4_ = bf16[12,2,64,256]{3,2,1,0:T(8,128)(2,1)} collective-permute-done((bf16[12,2,64,256]{3,2,1,0:T(8,128)(2,1)S(1)}, bf16[12,2,64,256]{3,2,1,0:T(8,128)(2,1)}, u32[]{:S(2)}, u32[]{:S(2)}) %collective-permute-start.16) | collective-permute-done | bytes 786464 | tf_op jit(solution)/shard_map/ppermute | solution.py:251
  40.5 1.8 %collective-permute-start.1 = (bf16[12,2,64,256]{3,2,1,0:T(8,128)(2,1)S(1)}, bf16[12,2,64,256]{3,2,1,0:T(8,128)(2,1)}, u32[]{:S(2)}, u32[]{:S(2)}) collective-permute-start(bf16[12,2,64,256]{3,2,1,0:T(8,128)(2,1)S(1)} %collective-permute-done.refs_4_), channel_id=1, source_target_pairs={{0,2},{2,4},{4,6},{6,7},{7,5},{5,3},{3,1},{1,0},{8,10},{10,12},{12... | collective-permute-start | bytes 2359304 | tf_op jit(solution)/shard_map/ppermute | solution.py:251
  42.3 0.9 copy-done.2
  43.2 0.2 collective-permute-start.5
  43.4 0.9 copy-done.4
  44.4 0.9 copy-done.6
  45.2 0.9 copy-done.8
  46.1 1.8 %collective-permute-start.17 = (bf16[12,2,64,256]{3,2,1,0:T(8,128)(2,1)}, bf16[12,2,64,256]{3,2,1,0:T(8,128)(2,1)}, u32[]{:S(2)}, u32[]{:S(2)}) collective-permute-start(bf16[12,2,64,256]{3,2,1,0:T(8,128)(2,1)} %collective-permute-done.16.refs_4_), channel_id=1, source_target_pairs={{0,2},{2,4},{4,6},{6,7},{7,5},{5,3},{3,1},{1,0},{8,10},{10,12},{12... | collective-permute-start | bytes 2359304 | tf_op jit(solution)/shard_map/ppermute | solution.py:251
  47.9 0.9 copy-done.10
  48.8 0.2 collective-permute-start.20
  49.1 11.9 %collective-permute-done.1.refs_4_ = bf16[12,2,64,256]{3,2,1,0:T(8,128)(2,1)} collective-permute-done((bf16[12,2,64,256]{3,2,1,0:T(8,128)(2,1)S(1)}, bf16[12,2,64,256]{3,2,1,0:T(8,128)(2,1)}, u32[]{:S(2)}, u32[]{:S(2)}) %collective-permute-start.1) | collective-permute-done | bytes 786464 | tf_op jit(solution)/shard_map/ppermute | solution.py:251
  61.0 2.7 %collective-permute-done.5.refs_5_ = bf16[12,2,64,256]{3,2,1,0:T(8,128)(2,1)} collective-permute-done((bf16[12,2,64,256]{3,2,1,0:T(8,128)(2,1)S(1)}, bf16[12,2,64,256]{3,2,1,0:T(8,128)(2,1)}, u32[]{:S(2)}, u32[]{:S(2)}) %collective-permute-start.5) | collective-permute-done | bytes 786464 | tf_op jit(solution)/shard_map/ppermute | solution.py:251
  63.7 0.9 copy-done.12
  64.6 1.6 collective-permute-start.2
  66.2 0.8 pad_add_fusion
  67.0 0.1 dynamic_slice.10
  67.1 1.2 dynamic_slice.12
  68.3 0.6 fusion.1
  68.9 8.9 %collective-permute-done.17.refs_4_ = bf16[12,2,64,256]{3,2,1,0:T(8,128)(2,1)} collective-permute-done((bf16[12,2,64,256]{3,2,1,0:T(8,128)(2,1)}, bf16[12,2,64,256]{3,2,1,0:T(8,128)(2,1)}, u32[]{:S(2)}, u32[]{:S(2)}) %collective-permute-start.17) | collective-permute-done | bytes 786464 | tf_op jit(solution)/shard_map/ppermute | solution.py:251
  77.9 1.7 %collective-permute-start.6 = (bf16[12,2,64,256]{3,2,1,0:T(8,128)(2,1)}, bf16[12,2,64,256]{3,2,1,0:T(8,128)(2,1)}, u32[]{:S(2)}, u32[]{:S(2)}) collective-permute-start(bf16[12,2,64,256]{3,2,1,0:T(8,128)(2,1)} %collective-permute-done.5.refs_5_), channel_id=1, source_target_pairs={{2,0},{4,2},{6,4},{7,6},{5,7},{3,5},{1,3},{0,1},{10,8},{12,10},{14... | collective-permute-start | bytes 2359304 | tf_op jit(solution)/shard_map/ppermute | solution.py:251
  79.7 0.2 collective-permute-done.20.refs_5_
  79.8 0.5 collective-permute-start.27
  80.3 1.3 gather_fusion
  81.7 1.6 collective-permute-start.18
  83.3 11.4 %collective-permute-done.2.refs_4_ = bf16[12,2,64,256]{3,2,1,0:T(8,128)(2,1)} collective-permute-done((bf16[12,2,64,256]{3,2,1,0:T(8,128)(2,1)}, bf16[12,2,64,256]{3,2,1,0:T(8,128)(2,1)}, u32[]{:S(2)}, u32[]{:S(2)}) %collective-permute-start.2) | collective-permute-done | bytes 786464 | tf_op jit(solution)/shard_map/ppermute | solution.py:251
  94.7 1.7 %collective-permute-start.21 = (bf16[12,2,64,256]{3,2,1,0:T(8,128)(2,1)}, bf16[12,2,64,256]{3,2,1,0:T(8,128)(2,1)}, u32[]{:S(2)}, u32[]{:S(2)}) collective-permute-start(bf16[12,2,64,256]{3,2,1,0:T(8,128)(2,1)} %collective-permute-done.20.refs_5_), channel_id=1, source_target_pairs={{2,0},{4,2},{6,4},{7,6},{5,7},{3,5},{1,3},{0,1},{10,8},{12,10},{14... | collective-permute-start | bytes 2359304 | tf_op jit(solution)/shard_map/ppermute | solution.py:251
  96.5 2.1 %fusion.4 = (bf16[12,2,32,256]{3,2,1,0:T(8,128)(2,1)}, bf16[12,2,32,256]{3,2,1,0:T(8,128)(2,1)}) fusion(bf16[12,2,64,256]{3,2,1,0:T(8,128)(2,1)} %collective-permute-done.2.refs_4_), kind=kLoop, calls=%fused_computation.17 | loop fusion | bytes 1572864 | tf_op jit(solution)/shard_map/slice | solution.py:250
  98.5 0.3 collective-permute-start.12
  98.8 2.1 %fusion.3 = (bf16[12,2,32,256]{3,2,1,0:T(8,128)(2,1)}, bf16[12,2,32,256]{3,2,1,0:T(8,128)(2,1)}) fusion(bf16[12,2,64,256]{3,2,1,0:T(8,128)(2,1)} %collective-permute-done.6.refs_5_), kind=kLoop, calls=%fused_computation.16 | loop fusion | bytes 1572864 | tf_op jit(solution)/shard_map/slice | solution.py:250
  100.9 1.7 %collective-permute-start.13 = (bf16[12,2,32,256]{3,2,1,0:T(8,128)(2,1)}, bf16[12,2,32,256]{3,2,1,0:T(8,128)(2,1)}, u32[]{:S(2)}, u32[]{:S(2)}) collective-permute-start(bf16[12,2,32,256]{3,2,1,0:T(8,128)(2,1)} %get-tuple-element.15), channel_id=1, source_target_pairs={{2,0},{4,2},{6,4},{7,6},{5,7},{3,5},{1,3},{0,1},{10,8},{12,10},{14... | collective-permute-start | bytes 1179656 | tf_op jit(solution)/shard_map/ppermute | solution.py:251
  102.6 0.3 collective-permute-start.3
  102.9 8.6 %collective-permute-done.18.refs_4_ = bf16[12,2,64,256]{3,2,1,0:T(8,128)(2,1)} collective-permute-done((bf16[12,2,64,256]{3,2,1,0:T(8,128)(2,1)}, bf16[12,2,64,256]{3,2,1,0:T(8,128)(2,1)}, u32[]{:S(2)}, u32[]{:S(2)}) %collective-permute-start.18) | collective-permute-done | bytes 786464 | tf_op jit(solution)/shard_map/ppermute | solution.py:251
  111.6 0.1 dynamic-slice_bitcast_fusion
  111.6 0.1 add.109
  111.7 0.1 copy.36.own_vir
  111.8 0.6 gather_fusion.1
  112.4 7.2 %gather_fusion.2 = s32[1152]{0:T(1024)S(1)} fusion(s32[16,128]{1,0:T(8,128)S(1)} %gather_fusion.1, s32[1152]{0:T(1024)S(1)} %copy-done.14), kind=kCustom, calls=%fused_computation.2 | custom fusion | bytes 18432 | tf_op jit(solution)/shard_map/gather | solution.py:268
  119.6 0.6 collective-permute-start.25
  120.2 0.1 collective-permute-start.22
  120.3 0.1 broadcast_in_dim.10.occ_pairs
  120.4 3.4 %shard_map.91.refs_8_ = f32[2,128,3072]{2,1,0:T(8,128)S(1)} custom-call(s32[8,1,128]{2,1,0:T(1,128)S(1)} %broadcast_in_dim.10.occ_pairs, s32[128,1]{1,0:T(8,128)S(1)} %copy.36.own_vir, s32[9,1,128]{2,1,0:T(1,128)S(1)} %broadcast_in_dim.25.vir_rows, bf16[12,2,64,256]{3,2,1,0:T(8,128)(2,1)S(1)} %get-tuple-element.10.refs_0_, ...), custom_call_target="tpu_custom_call" | custom-call | flops 2013265920 | bytes 12582912 | tf_op jit(solution)/shard_map/pallas_call | solution.py:207
  123.9 2.0 %collective-permute-start.7 = (bf16[12,2,32,256]{3,2,1,0:T(8,128)(2,1)S(1)}, bf16[12,2,32,256]{3,2,1,0:T(8,128)(2,1)S(1)}, u32[]{:S(2)}, u32[]{:S(2)}) collective-permute-start(bf16[12,2,32,256]{3,2,1,0:T(8,128)(2,1)S(1)} %copy-done.15), channel_id=1, source_target_pairs={{2,0},{4,2},{6,4},{7,6},{5,7},{3,5},{1,3},{0,1},{10,8},{12,10},{14... | collective-permute-start | bytes 1179656 | tf_op jit(solution)/shard_map/ppermute | solution.py:251
  125.8 2.1 %collective-permute-done.3.refs_4_.refs_2_ = bf16[12,2,32,256]{3,2,1,0:T(8,128)(2,1)} collective-permute-done((bf16[12,2,32,256]{3,2,1,0:T(8,128)(2,1)}, bf16[12,2,32,256]{3,2,1,0:T(8,128)(2,1)}, u32[]{:S(2)}, u32[]{:S(2)}) %collective-permute-start.3) | collective-permute-done | bytes 393248 | tf_op jit(solution)/shard_map/ppermute | solution.py:251
  128.0 3.7 %shard_map.92.refs_8_ = f32[2,128,3072]{2,1,0:T(8,128)S(1)} custom-call(s32[8,1,128]{2,1,0:T(1,128)S(1)} %broadcast_in_dim.10.occ_pairs, s32[128,1]{1,0:T(8,128)S(1)} %copy.36.own_vir, s32[9,1,128]{2,1,0:T(1,128)S(1)} %broadcast_in_dim.25.vir_rows, bf16[12,2,64,256]{3,2,1,0:T(8,128)(2,1)S(1)} %get-tuple-element.10.refs_0_, ...), custom_call_target="tpu_custom_call", output_to_operand_aliasing={{}: (11, {})} | custom-call | flops 2013265920 | bytes 12582912 | tf_op jit(solution)/shard_map/pallas_call | solution.py:207
  131.7 5.1 %shard_map.93.refs_8_ = f32[2,128,3072]{2,1,0:T(8,128)S(1)} custom-call(s32[8,1,128]{2,1,0:T(1,128)S(1)} %broadcast_in_dim.10.occ_pairs, s32[128,1]{1,0:T(8,128)S(1)} %copy.36.own_vir, s32[9,1,128]{2,1,0:T(1,128)S(1)} %broadcast_in_dim.25.vir_rows, bf16[12,2,64,256]{3,2,1,0:T(8,128)(2,1)S(1)} %get-tuple-element.10.refs_0_, ...), custom_call_target="tpu_custom_call", output_to_operand_aliasing={{}: (11, {})} | custom-call | flops 2013265920 | bytes 12582912 | tf_op jit(solution)/shard_map/pallas_call | solution.py:207
  136.8 5.6 %shard_map.94.refs_8_ = f32[2,128,3072]{2,1,0:T(8,128)S(1)} custom-call(s32[8,1,128]{2,1,0:T(1,128)S(1)} %broadcast_in_dim.10.occ_pairs, s32[128,1]{1,0:T(8,128)S(1)} %copy.36.own_vir, s32[9,1,128]{2,1,0:T(1,128)S(1)} %broadcast_in_dim.25.vir_rows, bf16[12,2,64,256]{3,2,1,0:T(8,128)(2,1)S(1)} %get-tuple-element.10.refs_0_, ...), custom_call_target="tpu_custom_call", output_to_operand_aliasing={{}: (11, {})} | custom-call | flops 2013265920 | bytes 12582912 | tf_op jit(solution)/shard_map/pallas_call | solution.py:207
  142.4 0.6 collective-permute-start.14
  142.9 0.1 collective-permute-start.15
  143.0 5.5 %shard_map.95.refs_8_ = f32[2,128,3072]{2,1,0:T(8,128)S(1)} custom-call(s32[8,1,128]{2,1,0:T(1,128)S(1)} %broadcast_in_dim.10.occ_pairs, s32[128,1]{1,0:T(8,128)S(1)} %copy.36.own_vir, s32[9,1,128]{2,1,0:T(1,128)S(1)} %broadcast_in_dim.25.vir_rows, bf16[12,2,64,256]{3,2,1,0:T(8,128)(2,1)S(1)} %get-tuple-element.10.refs_0_, ...), custom_call_target="tpu_custom_call", output_to_operand_aliasing={{}: (11, {})} | custom-call | flops 2013265920 | bytes 12582912 | tf_op jit(solution)/shard_map/pallas_call | solution.py:207
  148.6 0.5 collective-permute-start.8
  149.1 0.1 collective-permute-start.9
  149.2 5.3 %shard_map.96.refs_8_ = f32[2,128,3072]{2,1,0:T(8,128)S(1)} custom-call(s32[8,1,128]{2,1,0:T(1,128)S(1)} %broadcast_in_dim.10.occ_pairs, s32[128,1]{1,0:T(8,128)S(1)} %copy.36.own_vir, s32[9,1,128]{2,1,0:T(1,128)S(1)} %broadcast_in_dim.25.vir_rows, bf16[12,2,64,256]{3,2,1,0:T(8,128)(2,1)S(1)} %get-tuple-element.10.refs_0_, ...), custom_call_target="tpu_custom_call", output_to_operand_aliasing={{}: (11, {})} | custom-call | flops 2013265920 | bytes 12582912 | tf_op jit(solution)/shard_map/pallas_call | solution.py:207
  154.5 5.1 %shard_map.97.refs_8_ = f32[2,128,3072]{2,1,0:T(8,128)S(1)} custom-call(s32[8,1,128]{2,1,0:T(1,128)S(1)} %broadcast_in_dim.10.occ_pairs, s32[128,1]{1,0:T(8,128)S(1)} %copy.36.own_vir, s32[9,1,128]{2,1,0:T(1,128)S(1)} %broadcast_in_dim.25.vir_rows, bf16[12,2,64,256]{3,2,1,0:T(8,128)(2,1)S(1)} %get-tuple-element.10.refs_0_, ...), custom_call_target="tpu_custom_call", output_to_operand_aliasing={{}: (11, {})} | custom-call | flops 2013265920 | bytes 12582912 | tf_op jit(solution)/shard_map/pallas_call | solution.py:207
  159.6 4.6 %shard_map.98.refs_6_ = f32[2,128,3072]{2,1,0:T(8,128)S(1)} custom-call(s32[8,1,128]{2,1,0:T(1,128)S(1)} %broadcast_in_dim.10.occ_pairs, s32[128,1]{1,0:T(8,128)S(1)} %copy.36.own_vir, s32[9,1,128]{2,1,0:T(1,128)S(1)} %broadcast_in_dim.25.vir_rows, bf16[12,2,64,256]{3,2,1,0:T(8,128)(2,1)S(1)} %get-tuple-element.10.refs_0_, ...), custom_call_target="tpu_custom_call", output_to_operand_aliasing={{}: (11, {})} | custom-call | flops 1006632960 | bytes 11010048 | tf_op jit(solution)/shard_map/pallas_call | solution.py:207
  164.2 2.4 %shard_map.99 = (bf16[256,128]{1,0:T(8,128)(2,1)S(1)}, bf16[256,128]{1,0:T(8,128)(2,1)S(1)}, f32[2,128,3072]{2,1,0:T(8,128)S(1)}) custom-call(s32[8,1,128]{2,1,0:T(1,128)S(1)} %broadcast_in_dim.10.occ_pairs, s32[128,1]{1,0:T(8,128)S(1)} %copy.36.own_vir, s32[9,1,128]{2,1,0:T(1,128)S(1)} %broadcast_in_dim.25.vir_rows, ...), custom_call_target="tpu_custom_call" | custom-call | flops 402653184 | bytes 11010048 | tf_op jit(solution)/shard_map/pallas_call | solution.py:207
  166.6 3.9 %shard_map.100 = f32[2,128,3072]{2,1,0:T(8,128)} custom-call(s32[8,1,128]{2,1,0:T(1,128)S(1)} %broadcast_in_dim.10.occ_pairs, s32[128,1]{1,0:T(8,128)S(1)} %copy.36.own_vir, s32[9,1,128]{2,1,0:T(1,128)S(1)} %broadcast_in_dim.25.vir_rows, bf16[12,2,64,256]{3,2,1,0:T(8,128)(2,1)S(1)} %get-tuple-element.10.refs_0_, ...), custom_call_target="tpu_custom_call" | custom-call | flops 603979776 | bytes 11010048 | tf_op jit(solution)/shard_map/pallas_call | solution.py:207
  (65 shorter events, 0.2 us)
Async XLA Ops:
  0.0 111.6 %copy-start = (s32[1024]{0:T(1024)S(1)}, s32[1024]{0:T(1024)}, u32[]{:S(2)}) copy-start(s32[1024]{0:T(1024)} %param.11) | copy-start | bytes 12292
  0.0 1.4 copy-start.1
  1.4 111.0 %copy-start.14 = (s32[1152]{0:T(1024)S(1)}, s32[1152]{0:T(1024)}, u32[]{:S(2)}) copy-start(s32[1152]{0:T(1024)} %constant.98) | copy-start | bytes 13828
  2.2 5.2 %collective-permute-start.10 = (bf16[12,2,64,256]{3,2,1,0:T(8,128)(2,1)S(1)}, bf16[12,2,64,256]{3,2,1,0:T(8,128)(2,1)S(1)}, u32[]{:S(2)}, u32[]{:S(2)}) collective-permute-start(bf16[12,2,64,256]{3,2,1,0:T(8,128)(2,1)S(1)} %get-tuple-element.10.refs_0_), channel_id=1, source_target_pairs={{8,0},{0,8},{9,1},{1,9},{10,2},{2,10},{11,3},{3,11},{12,4},{4,12},... | collective-permute-start | bytes 2359304 | tf_op jit(solution)/shard_map/ppermute | solution.py:238
  2.8 21.0 %collective-permute-start = (bf16[12,2,64,256]{3,2,1,0:T(8,128)(2,1)S(1)}, bf16[12,2,64,256]{3,2,1,0:T(8,128)(2,1)S(1)}, u32[]{:S(2)}, u32[]{:S(2)}) collective-permute-start(bf16[12,2,64,256]{3,2,1,0:T(8,128)(2,1)S(1)} %get-tuple-element.10.refs_0_), channel_id=1, source_target_pairs={{0,2},{2,4},{4,6},{6,7},{7,5},{5,3},{3,1},{1,0},{8,10},{10,12},{12... | collective-permute-start | bytes 2359304 | tf_op jit(solution)/shard_map/ppermute | solution.py:251
  5.4 20.4 %collective-permute-start.4 = (bf16[12,2,64,256]{3,2,1,0:T(8,128)(2,1)S(1)}, bf16[12,2,64,256]{3,2,1,0:T(8,128)(2,1)S(1)}, u32[]{:S(2)}, u32[]{:S(2)}) collective-permute-start(bf16[12,2,64,256]{3,2,1,0:T(8,128)(2,1)S(1)} %get-tuple-element.11.refs_1_), channel_id=1, source_target_pairs={{2,0},{4,2},{6,4},{7,6},{5,7},{3,5},{1,3},{0,1},{10,8},{12,10},{14... | collective-permute-start | bytes 2359304 | tf_op jit(solution)/shard_map/ppermute | solution.py:251
  5.4 35.0 %collective-permute-start.16 = (bf16[12,2,64,256]{3,2,1,0:T(8,128)(2,1)S(1)}, bf16[12,2,64,256]{3,2,1,0:T(8,128)(2,1)}, u32[]{:S(2)}, u32[]{:S(2)}) collective-permute-start(bf16[12,2,64,256]{3,2,1,0:T(8,128)(2,1)S(1)} %get-tuple-element.11.refs_1_), channel_id=1, source_target_pairs={{0,2},{2,4},{4,6},{6,7},{7,5},{5,3},{3,1},{1,0},{8,10},{10,12},{12... | collective-permute-start | bytes 2359304 | tf_op jit(solution)/shard_map/ppermute | solution.py:251
  7.4 33.0 %collective-permute-start.11 = (bf16[12,2,64,256]{3,2,1,0:T(8,128)(2,1)S(1)}, bf16[12,2,64,256]{3,2,1,0:T(8,128)(2,1)S(1)}, u32[]{:S(2)}, u32[]{:S(2)}) collective-permute-start(bf16[12,2,64,256]{3,2,1,0:T(8,128)(2,1)S(1)} %get-tuple-element.11.refs_1_), channel_id=1, source_target_pairs={{8,0},{0,8},{9,1},{1,9},{10,2},{2,10},{11,3},{3,11},{12,4},{4,12},... | collective-permute-start | bytes 2359304 | tf_op jit(solution)/shard_map/ppermute | solution.py:238
  7.5 35.7 %collective-permute-start.19 = (bf16[12,2,64,256]{3,2,1,0:T(8,128)(2,1)S(1)}, bf16[12,2,64,256]{3,2,1,0:T(8,128)(2,1)}, u32[]{:S(2)}, u32[]{:S(2)}) collective-permute-start(bf16[12,2,64,256]{3,2,1,0:T(8,128)(2,1)S(1)} %get-tuple-element.10.refs_0_), channel_id=1, source_target_pairs={{2,0},{4,2},{6,4},{7,6},{5,7},{3,5},{1,3},{0,1},{10,8},{12,10},{14... | collective-permute-start | bytes 2359304 | tf_op jit(solution)/shard_map/ppermute | solution.py:251
  23.8 20.6 %collective-permute-start.32 = (bf16[12,2,64,256]{3,2,1,0:T(8,128)(2,1)S(1)}, bf16[12,2,64,256]{3,2,1,0:T(8,128)(2,1)S(1)}, u32[]{:S(2)}, u32[]{:S(2)}) collective-permute-start(bf16[12,2,64,256]{3,2,1,0:T(8,128)(2,1)S(1)} %collective-permute-done.refs_4_), channel_id=1, source_target_pairs={{8,0},{0,8},{9,1},{1,9},{10,2},{2,10},{11,3},{3,11},{12,4},{4,12},... | collective-permute-start | bytes 2359304 | tf_op jit(solution)/shard_map/ppermute | solution.py:256
  25.8 19.4 %collective-permute-start.33 = (bf16[12,2,64,256]{3,2,1,0:T(8,128)(2,1)S(1)}, bf16[12,2,64,256]{3,2,1,0:T(8,128)(2,1)S(1)}, u32[]{:S(2)}, u32[]{:S(2)}) collective-permute-start(bf16[12,2,64,256]{3,2,1,0:T(8,128)(2,1)S(1)} %collective-permute-done.4.refs_5_), channel_id=1, source_target_pairs={{8,0},{0,8},{9,1},{1,9},{10,2},{2,10},{11,3},{3,11},{12,4},{4,12},... | collective-permute-start | bytes 2359304 | tf_op jit(solution)/shard_map/ppermute | solution.py:256
  40.5 7.5 %collective-permute-start.30 = (bf16[12,2,64,256]{3,2,1,0:T(8,128)(2,1)}, bf16[12,2,64,256]{3,2,1,0:T(8,128)(2,1)S(1)}, u32[]{:S(2)}, u32[]{:S(2)}) collective-permute-start(bf16[12,2,64,256]{3,2,1,0:T(8,128)(2,1)} %collective-permute-done.16.refs_4_), channel_id=1, source_target_pairs={{8,0},{0,8},{9,1},{1,9},{10,2},{2,10},{11,3},{3,11},{12,4},{4,12},... | collective-permute-start | bytes 2359304 | tf_op jit(solution)/shard_map/ppermute | solution.py:256
  40.5 20.5 %collective-permute-start.1 = (bf16[12,2,64,256]{3,2,1,0:T(8,128)(2,1)S(1)}, bf16[12,2,64,256]{3,2,1,0:T(8,128)(2,1)}, u32[]{:S(2)}, u32[]{:S(2)}) collective-permute-start(bf16[12,2,64,256]{3,2,1,0:T(8,128)(2,1)S(1)} %collective-permute-done.refs_4_), channel_id=1, source_target_pairs={{0,2},{2,4},{4,6},{6,7},{7,5},{5,3},{3,1},{1,0},{8,10},{10,12},{12... | collective-permute-start | bytes 2359304 | tf_op jit(solution)/shard_map/ppermute | solution.py:251
  42.3 0.9 copy-start.2
  43.2 20.5 %collective-permute-start.5 = (bf16[12,2,64,256]{3,2,1,0:T(8,128)(2,1)S(1)}, bf16[12,2,64,256]{3,2,1,0:T(8,128)(2,1)}, u32[]{:S(2)}, u32[]{:S(2)}) collective-permute-start(bf16[12,2,64,256]{3,2,1,0:T(8,128)(2,1)S(1)} %collective-permute-done.4.refs_5_), channel_id=1, source_target_pairs={{2,0},{4,2},{6,4},{7,6},{5,7},{3,5},{1,3},{0,1},{10,8},{12,10},{14... | collective-permute-start | bytes 2359304 | tf_op jit(solution)/shard_map/ppermute | solution.py:251
  43.4 0.9 copy-start.4
  44.4 0.9 copy-start.6
  45.2 18.5 %collective-permute-start.31 = (bf16[12,2,64,256]{3,2,1,0:T(8,128)(2,1)}, bf16[12,2,64,256]{3,2,1,0:T(8,128)(2,1)S(1)}, u32[]{:S(2)}, u32[]{:S(2)}) collective-permute-start(bf16[12,2,64,256]{3,2,1,0:T(8,128)(2,1)} %collective-permute-done.19.refs_5_), channel_id=1, source_target_pairs={{8,0},{0,8},{9,1},{1,9},{10,2},{2,10},{11,3},{3,11},{12,4},{4,12},... | collective-permute-start | bytes 2359304 | tf_op jit(solution)/shard_map/ppermute | solution.py:256
  45.2 0.9 copy-start.8
  46.1 31.7 %collective-permute-start.17 = (bf16[12,2,64,256]{3,2,1,0:T(8,128)(2,1)}, bf16[12,2,64,256]{3,2,1,0:T(8,128)(2,1)}, u32[]{:S(2)}, u32[]{:S(2)}) collective-permute-start(bf16[12,2,64,256]{3,2,1,0:T(8,128)(2,1)} %collective-permute-done.16.refs_4_), channel_id=1, source_target_pairs={{0,2},{2,4},{4,6},{6,7},{7,5},{5,3},{3,1},{1,0},{8,10},{10,12},{12... | collective-permute-start | bytes 2359304 | tf_op jit(solution)/shard_map/ppermute | solution.py:251
  47.9 0.9 copy-start.10
  48.8 31.0 %collective-permute-start.20 = (bf16[12,2,64,256]{3,2,1,0:T(8,128)(2,1)}, bf16[12,2,64,256]{3,2,1,0:T(8,128)(2,1)}, u32[]{:S(2)}, u32[]{:S(2)}) collective-permute-start(bf16[12,2,64,256]{3,2,1,0:T(8,128)(2,1)} %collective-permute-done.19.refs_5_), channel_id=1, source_target_pairs={{2,0},{4,2},{6,4},{7,6},{5,7},{3,5},{1,3},{0,1},{10,8},{12,10},{14... | collective-permute-start | bytes 2359304 | tf_op jit(solution)/shard_map/ppermute | solution.py:251
  61.0 18.8 %collective-permute-start.28 = (bf16[12,2,64,256]{3,2,1,0:T(8,128)(2,1)}, bf16[12,2,64,256]{3,2,1,0:T(8,128)(2,1)}, u32[]{:S(2)}, u32[]{:S(2)}) collective-permute-start(bf16[12,2,64,256]{3,2,1,0:T(8,128)(2,1)} %collective-permute-done.1.refs_4_), channel_id=1, source_target_pairs={{8,0},{0,8},{9,1},{1,9},{10,2},{2,10},{11,3},{3,11},{12,4},{4,12},... | collective-permute-start | bytes 2359304 | tf_op jit(solution)/shard_map/ppermute | solution.py:256
  63.7 17.9 %collective-permute-start.29 = (bf16[12,2,64,256]{3,2,1,0:T(8,128)(2,1)}, bf16[12,2,64,256]{3,2,1,0:T(8,128)(2,1)}, u32[]{:S(2)}, u32[]{:S(2)}) collective-permute-start(bf16[12,2,64,256]{3,2,1,0:T(8,128)(2,1)} %collective-permute-done.5.refs_5_), channel_id=1, source_target_pairs={{8,0},{0,8},{9,1},{1,9},{10,2},{2,10},{11,3},{3,11},{12,4},{4,12},... | collective-permute-start | bytes 2359304 | tf_op jit(solution)/shard_map/ppermute | solution.py:256
  63.7 0.9 copy-start.12
  64.6 30.1 %collective-permute-start.2 = (bf16[12,2,64,256]{3,2,1,0:T(8,128)(2,1)}, bf16[12,2,64,256]{3,2,1,0:T(8,128)(2,1)}, u32[]{:S(2)}, u32[]{:S(2)}) collective-permute-start(bf16[12,2,64,256]{3,2,1,0:T(8,128)(2,1)} %collective-permute-done.1.refs_4_), channel_id=1, source_target_pairs={{0,2},{2,4},{4,6},{6,7},{7,5},{5,3},{3,1},{1,0},{8,10},{10,12},{12... | collective-permute-start | bytes 2359304 | tf_op jit(solution)/shard_map/ppermute | solution.py:251
  77.9 20.7 %collective-permute-start.6 = (bf16[12,2,64,256]{3,2,1,0:T(8,128)(2,1)}, bf16[12,2,64,256]{3,2,1,0:T(8,128)(2,1)}, u32[]{:S(2)}, u32[]{:S(2)}) collective-permute-start(bf16[12,2,64,256]{3,2,1,0:T(8,128)(2,1)} %collective-permute-done.5.refs_5_), channel_id=1, source_target_pairs={{2,0},{4,2},{6,4},{7,6},{5,7},{3,5},{1,3},{0,1},{10,8},{12,10},{14... | collective-permute-start | bytes 2359304 | tf_op jit(solution)/shard_map/ppermute | solution.py:251
  79.8 21.1 %collective-permute-start.26 = (bf16[12,2,64,256]{3,2,1,0:T(8,128)(2,1)}, bf16[12,2,64,256]{3,2,1,0:T(8,128)(2,1)}, u32[]{:S(2)}, u32[]{:S(2)}) collective-permute-start(bf16[12,2,64,256]{3,2,1,0:T(8,128)(2,1)} %collective-permute-done.17.refs_4_), channel_id=1, source_target_pairs={{8,0},{0,8},{9,1},{1,9},{10,2},{2,10},{11,3},{3,11},{12,4},{4,12},... | collective-permute-start | bytes 2359304 | tf_op jit(solution)/shard_map/ppermute | solution.py:256
  79.8 22.8 %collective-permute-start.27 = (bf16[12,2,64,256]{3,2,1,0:T(8,128)(2,1)}, bf16[12,2,64,256]{3,2,1,0:T(8,128)(2,1)}, u32[]{:S(2)}, u32[]{:S(2)}) collective-permute-start(bf16[12,2,64,256]{3,2,1,0:T(8,128)(2,1)} %collective-permute-done.20.refs_5_), channel_id=1, source_target_pairs={{8,0},{0,8},{9,1},{1,9},{10,2},{2,10},{11,3},{3,11},{12,4},{4,12},... | collective-permute-start | bytes 2359304 | tf_op jit(solution)/shard_map/ppermute | solution.py:256
  81.7 29.9 %collective-permute-start.18 = (bf16[12,2,64,256]{3,2,1,0:T(8,128)(2,1)}, bf16[12,2,64,256]{3,2,1,0:T(8,128)(2,1)}, u32[]{:S(2)}, u32[]{:S(2)}) collective-permute-start(bf16[12,2,64,256]{3,2,1,0:T(8,128)(2,1)} %collective-permute-done.17.refs_4_), channel_id=1, source_target_pairs={{0,2},{2,4},{4,6},{6,7},{7,5},{5,3},{3,1},{1,0},{8,10},{10,12},{12... | collective-permute-start | bytes 2359304 | tf_op jit(solution)/shard_map/ppermute | solution.py:251
  94.7 24.9 %collective-permute-start.21 = (bf16[12,2,64,256]{3,2,1,0:T(8,128)(2,1)}, bf16[12,2,64,256]{3,2,1,0:T(8,128)(2,1)}, u32[]{:S(2)}, u32[]{:S(2)}) collective-permute-start(bf16[12,2,64,256]{3,2,1,0:T(8,128)(2,1)} %collective-permute-done.20.refs_5_), channel_id=1, source_target_pairs={{2,0},{4,2},{6,4},{7,6},{5,7},{3,5},{1,3},{0,1},{10,8},{12,10},{14... | collective-permute-start | bytes 2359304 | tf_op jit(solution)/shard_map/ppermute | solution.py:251
  98.5 21.7 %collective-permute-start.12 = (bf16[12,2,32,256]{3,2,1,0:T(8,128)(2,1)}, bf16[12,2,32,256]{3,2,1,0:T(8,128)(2,1)}, u32[]{:S(2)}, u32[]{:S(2)}) collective-permute-start(bf16[12,2,32,256]{3,2,1,0:T(8,128)(2,1)} %get-tuple-element.17), channel_id=1, source_target_pairs={{0,2},{2,4},{4,6},{6,7},{7,5},{5,3},{3,1},{1,0},{8,10},{10,12},{12... | collective-permute-start | bytes 1179656 | tf_op jit(solution)/shard_map/ppermute | solution.py:251
  100.9 22.9 %collective-permute-start.13 = (bf16[12,2,32,256]{3,2,1,0:T(8,128)(2,1)}, bf16[12,2,32,256]{3,2,1,0:T(8,128)(2,1)}, u32[]{:S(2)}, u32[]{:S(2)}) collective-permute-start(bf16[12,2,32,256]{3,2,1,0:T(8,128)(2,1)} %get-tuple-element.15), channel_id=1, source_target_pairs={{2,0},{4,2},{6,4},{7,6},{5,7},{3,5},{1,3},{0,1},{10,8},{12,10},{14... | collective-permute-start | bytes 1179656 | tf_op jit(solution)/shard_map/ppermute | solution.py:251
  102.6 25.3 %collective-permute-start.3 = (bf16[12,2,32,256]{3,2,1,0:T(8,128)(2,1)}, bf16[12,2,32,256]{3,2,1,0:T(8,128)(2,1)}, u32[]{:S(2)}, u32[]{:S(2)}) collective-permute-start(bf16[12,2,32,256]{3,2,1,0:T(8,128)(2,1)} %get-tuple-element.18), channel_id=1, source_target_pairs={{0,2},{2,4},{4,6},{6,7},{7,5},{5,3},{3,1},{1,0},{8,10},{10,12},{12... | collective-permute-start | bytes 1179656 | tf_op jit(solution)/shard_map/ppermute | solution.py:251
  111.6 31.4 %collective-permute-start.24 = (bf16[12,2,64,256]{3,2,1,0:T(8,128)(2,1)}, bf16[12,2,64,256]{3,2,1,0:T(8,128)(2,1)}, u32[]{:S(2)}, u32[]{:S(2)}) collective-permute-start(bf16[12,2,64,256]{3,2,1,0:T(8,128)(2,1)} %collective-permute-done.2.refs_4_), channel_id=1, source_target_pairs={{8,0},{0,8},{9,1},{1,9},{10,2},{2,10},{11,3},{3,11},{12,4},{4,12},... | collective-permute-start | bytes 2359304 | tf_op jit(solution)/shard_map/ppermute | solution.py:256
  119.6 28.9 %collective-permute-start.25 = (bf16[12,2,64,256]{3,2,1,0:T(8,128)(2,1)}, bf16[12,2,64,256]{3,2,1,0:T(8,128)(2,1)S(1)}, u32[]{:S(2)}, u32[]{:S(2)}) collective-permute-start(bf16[12,2,64,256]{3,2,1,0:T(8,128)(2,1)} %collective-permute-done.6.refs_5_), channel_id=1, source_target_pairs={{8,0},{0,8},{9,1},{1,9},{10,2},{2,10},{11,3},{3,11},{12,4},{4,12},... | collective-permute-start | bytes 2359304 | tf_op jit(solution)/shard_map/ppermute | solution.py:256
  120.2 28.9 %collective-permute-start.22 = (bf16[12,2,64,256]{3,2,1,0:T(8,128)(2,1)}, bf16[12,2,64,256]{3,2,1,0:T(8,128)(2,1)S(1)}, u32[]{:S(2)}, u32[]{:S(2)}) collective-permute-start(bf16[12,2,64,256]{3,2,1,0:T(8,128)(2,1)} %collective-permute-done.18.refs_4_), channel_id=1, source_target_pairs={{8,0},{0,8},{9,1},{1,9},{10,2},{2,10},{11,3},{3,11},{12,4},{4,12},... | collective-permute-start | bytes 2359304 | tf_op jit(solution)/shard_map/ppermute | solution.py:256
  120.4 3.5 %copy-start.15 = (bf16[12,2,32,256]{3,2,1,0:T(8,128)(2,1)S(1)}, bf16[12,2,32,256]{3,2,1,0:T(8,128)(2,1)}, u32[]{:S(2)}) copy-start(bf16[12,2,32,256]{3,2,1,0:T(8,128)(2,1)} %get-tuple-element.16) | copy-start | bytes 1179652
  120.4 7.6 %copy-start.3 = (bf16[12,2,64,256]{3,2,1,0:T(8,128)(2,1)S(1)}, bf16[12,2,64,256]{3,2,1,0:T(8,128)(2,1)}, u32[]{:S(2)}) copy-start(bf16[12,2,64,256]{3,2,1,0:T(8,128)(2,1)} %copy-done.2) | copy-start | bytes 2359300
  120.4 7.6 %copy-start.5 = (bf16[12,2,64,256]{3,2,1,0:T(8,128)(2,1)S(1)}, bf16[12,2,64,256]{3,2,1,0:T(8,128)(2,1)}, u32[]{:S(2)}) copy-start(bf16[12,2,64,256]{3,2,1,0:T(8,128)(2,1)} %copy-done.4) | copy-start | bytes 2359300
  120.4 7.6 %copy-start.7 = (bf16[12,2,64,256]{3,2,1,0:T(8,128)(2,1)S(1)}, bf16[12,2,64,256]{3,2,1,0:T(8,128)(2,1)}, u32[]{:S(2)}) copy-start(bf16[12,2,64,256]{3,2,1,0:T(8,128)(2,1)} %copy-done.6) | copy-start | bytes 2359300
  120.4 7.6 %copy-start.9 = (bf16[12,2,64,256]{3,2,1,0:T(8,128)(2,1)S(1)}, bf16[12,2,64,256]{3,2,1,0:T(8,128)(2,1)}, u32[]{:S(2)}) copy-start(bf16[12,2,64,256]{3,2,1,0:T(8,128)(2,1)} %copy-done.8) | copy-start | bytes 2359300
  123.8 7.9 %copy-start.11 = (bf16[12,2,64,256]{3,2,1,0:T(8,128)(2,1)S(1)}, bf16[12,2,64,256]{3,2,1,0:T(8,128)(2,1)}, u32[]{:S(2)}) copy-start(bf16[12,2,64,256]{3,2,1,0:T(8,128)(2,1)} %copy-done.10) | copy-start | bytes 2359300
  123.9 7.9 %copy-start.13 = (bf16[12,2,64,256]{3,2,1,0:T(8,128)(2,1)S(1)}, bf16[12,2,64,256]{3,2,1,0:T(8,128)(2,1)}, u32[]{:S(2)}) copy-start(bf16[12,2,64,256]{3,2,1,0:T(8,128)(2,1)} %copy-done.12) | copy-start | bytes 2359300
  123.9 18.5 %collective-permute-start.7 = (bf16[12,2,32,256]{3,2,1,0:T(8,128)(2,1)S(1)}, bf16[12,2,32,256]{3,2,1,0:T(8,128)(2,1)S(1)}, u32[]{:S(2)}, u32[]{:S(2)}) collective-permute-start(bf16[12,2,32,256]{3,2,1,0:T(8,128)(2,1)S(1)} %copy-done.15), channel_id=1, source_target_pairs={{2,0},{4,2},{6,4},{7,6},{5,7},{3,5},{1,3},{0,1},{10,8},{12,10},{14... | collective-permute-start | bytes 1179656 | tf_op jit(solution)/shard_map/ppermute | solution.py:251
  128.0 26.5 %collective-permute-start.23 = (bf16[12,2,64,256]{3,2,1,0:T(8,128)(2,1)}, bf16[12,2,64,256]{3,2,1,0:T(8,128)(2,1)S(1)}, u32[]{:S(2)}, u32[]{:S(2)}) collective-permute-start(bf16[12,2,64,256]{3,2,1,0:T(8,128)(2,1)} %collective-permute-done.21.refs_5_), channel_id=1, source_target_pairs={{8,0},{0,8},{9,1},{1,9},{10,2},{2,10},{11,3},{3,11},{12,4},{4,12},... | collective-permute-start | bytes 2359304 | tf_op jit(solution)/shard_map/ppermute | solution.py:256
  142.4 17.2 %collective-permute-start.14 = (bf16[12,2,32,256]{3,2,1,0:T(8,128)(2,1)}, bf16[12,2,32,256]{3,2,1,0:T(8,128)(2,1)S(1)}, u32[]{:S(2)}, u32[]{:S(2)}) collective-permute-start(bf16[12,2,32,256]{3,2,1,0:T(8,128)(2,1)} %collective-permute-done.12.refs_4_), channel_id=1, source_target_pairs={{8,0},{0,8},{9,1},{1,9},{10,2},{2,10},{11,3},{3,11},{12,4},{4,12},... | collective-permute-start | bytes 1179656 | tf_op jit(solution)/shard_map/ppermute | solution.py:256
  142.9 16.7 %collective-permute-start.15 = (bf16[12,2,32,256]{3,2,1,0:T(8,128)(2,1)}, bf16[12,2,32,256]{3,2,1,0:T(8,128)(2,1)S(1)}, u32[]{:S(2)}, u32[]{:S(2)}) collective-permute-start(bf16[12,2,32,256]{3,2,1,0:T(8,128)(2,1)} %collective-permute-done.13.refs_5_), channel_id=1, source_target_pairs={{8,0},{0,8},{9,1},{1,9},{10,2},{2,10},{11,3},{3,11},{12,4},{4,12},... | collective-permute-start | bytes 1179656 | tf_op jit(solution)/shard_map/ppermute | solution.py:256
  148.6 18.0 %collective-permute-start.8 = (bf16[12,2,32,256]{3,2,1,0:T(8,128)(2,1)}, bf16[12,2,32,256]{3,2,1,0:T(8,128)(2,1)S(1)}, u32[]{:S(2)}, u32[]{:S(2)}) collective-permute-start(bf16[12,2,32,256]{3,2,1,0:T(8,128)(2,1)} %collective-permute-done.3.refs_4_.refs_2_), channel_id=1, source_target_pairs={{8,0},{0,8},{9,1},{1,9},{10,2},{2,10},{11,3},{3,11},{12,4},{4,12},... | collective-permute-start | bytes 1179656 | tf_op jit(solution)/shard_map/ppermute | solution.py:256
  149.1 17.5 %collective-permute-start.9 = (bf16[12,2,32,256]{3,2,1,0:T(8,128)(2,1)S(1)}, bf16[12,2,32,256]{3,2,1,0:T(8,128)(2,1)S(1)}, u32[]{:S(2)}, u32[]{:S(2)}) collective-permute-start(bf16[12,2,32,256]{3,2,1,0:T(8,128)(2,1)S(1)} %collective-permute-done.7.refs_5_.refs_3_), channel_id=1, source_target_pairs={{8,0},{0,8},{9,1},{1,9},{10,2},{2,10},{11,3},{3,11},{12,4},{4,12},... | collective-permute-start | bytes 1179656 | tf_op jit(solution)/shard_map/ppermute | solution.py:256
